TPU v7x, 256 devices: a whole 4x4x8 slice. The times are simulated.
256 devices in a mesh: radial: 64 (over x, z, core), phi: 4 (over y).
Axes of the slice: x: 4, y: 4, z: 8, core: 2. Of those that a mesh axis runs over, the one named last changes fastest.
Arguments:
- conserved: float32 [8, 512, 64, 128], P(None, 'radial', 'phi'), may hold values from -2.5 to 7, as said below
- core_mass: float32 [1], replicated, may hold values from 0.2 to 1
Outputs:
- advanced: float32 [8, 512, 64, 128], P(None, 'radial', 'phi')
- enclosed_mass: float32 [512], P('radial')
Inputs may be any that keep to these rules, and one draw needn't show every extreme that they name: conserved[0] (density) lies between 0.4 and 2.5; conserved[4] exceeds (conserved[1]^2 + conserved[2]^2 + conserved[3]^2)/(2 conserved[0]) by at least 0.6; the speeds |conserved[m]/conserved[0]| stay below 1; conserved[5..7] lie between 0 and conserved[0].
All inputs are finite; a program needn't handle non-finite values.
Results may differ from a plain program's by a relative error of at most 0.0003.
Values sent between devices are 32-bit elements; how exact they have to be, the bound alone decides.
A program may use at most 64 MiB of HBM per device.

v0:
```python
import functools
import math

import jax
import jax.numpy as jnp
import numpy as np
from jax import lax
from jax.experimental import pallas as pl
from jax.experimental.pallas import tpu as pltpu
from jax.sharding import PartitionSpec as P

ADIABATIC = 4.0 / 3.0
INNER_RADIUS = 1.0
OUTER_RADIUS = 2.0
COURANT = 0.4
GRAVITY_KICK = 0.004
MINIMUM_DENSITY = 0.05
PRESSURE_FLOOR = 0.01
MESH = pl.DeviceIdType.MESH
TILE = 8
PAD = 8


def step_sizes(radial_total, phi_total, theta_total):
    theta_step = math.pi / theta_total
    phi_step = 2.0 * math.pi / phi_total
    polar_width = INNER_RADIUS * math.sin(0.5 * theta_step) * phi_step
    radial_step = min(2.0 * polar_width, (OUTER_RADIUS - INNER_RADIUS) / radial_total)
    timestep = COURANT * min(radial_step, polar_width)
    return (radial_step, theta_step, phi_step, timestep)


def angle_tables(theta_cells, theta_step):
    step = np.float32(theta_step)
    centre = (np.arange(theta_cells, dtype=np.float32) + np.float32(0.5)) * step
    face = np.arange(theta_cells + 1, dtype=np.float32) * step
    sine = np.sin(centre.astype(np.float64))
    cosine = np.cos(centre.astype(np.float64))
    face_sine = np.sin(face.astype(np.float64))
    zero = np.zeros(theta_cells)
    rows = [sine, face_sine[:-1], face_sine[1:], cosine / sine, 1.0 / sine, zero, zero, zero]
    return np.stack(rows).astype(np.float32)


def half_slope(below, above):
    return 0.5 * (
        jnp.maximum(jnp.minimum(below, above), 0.0) + jnp.minimum(jnp.maximum(below, above), 0.0)
    )


def thermo(q):
    density = jnp.maximum(q[0], MINIMUM_DENSITY)
    inverse = 1.0 / density
    kinetic = 0.5 * (q[1] * q[1] + q[2] * q[2] + q[3] * q[3]) * inverse
    pressure = jnp.maximum((ADIABATIC - 1.0) * (q[4] - kinetic), PRESSURE_FLOOR * density)
    return density, inverse, pressure


def physical(q, component):
    _, inverse, pressure = thermo(q)
    normal = q[component] * inverse
    squared = ADIABATIC * pressure * inverse
    return normal, pressure, jnp.abs(normal) + squared * lax.rsqrt(squared)


def flux(left, right, component):
    left_v, left_p, left_a = physical(left, component)
    right_v, right_p, right_a = physical(right, component)
    signal = jnp.maximum(left_a, right_a)
    left_w = 0.5 * (left_v + signal)
    right_w = 0.5 * (right_v - signal)
    out = [a * left_w + b * right_w for a, b in zip(left, right)]
    out[component] = out[component] + 0.5 * (left_p + right_p)
    out[4] = out[4] + 0.5 * (left_p * left_v + right_p * right_v)
    return out


def two_faces(rows, component):
    lower_left, lower_right, upper_left, upper_right = [], [], [], []
    for a, b, c, d, e in zip(*rows):
        ab, bc, cd, de = b - a, c - b, d - c, e - d
        sb, sc, sd = half_slope(ab, bc), half_slope(bc, cd), half_slope(cd, de)
        lower_left.append(b + sb)
        lower_right.append(c - sc)
        upper_left.append(c + sc)
        upper_right.append(d - sd)
    return flux(lower_left, lower_right, component), flux(upper_left, upper_right, component)


def kernel(
    sizes,
    counts,
    core_ref,
    table_ref,
    input_ref,
    out_ref,
    mass_ref,
    first,
    second,
    edge,
    halo,
    part,
    slab_part,
    got,
    pull,
    table,
    core,
    load_sem,
    radial_send,
    radial_recv,
    phi_send,
    phi_recv,
    part_send,
    part_recv,
):
    radial_step, theta_step, phi_step, timestep = sizes
    slabs, wedges = counts
    variables, rows, cells, lanes = input_ref.shape
    tiles = cells // TILE
    strength = GRAVITY_KICK / timestep
    slab, wedge = lax.axis_index("radial"), lax.axis_index("phi")
    has_up, has_down = slab < slabs - 1, slab > 0

    load = pltpu.make_async_copy(
        input_ref, first.at[:, pl.ds(2, rows), pl.ds(PAD, cells), :], load_sem.at[0]
    )
    load.start()
    load_table = pltpu.make_async_copy(table_ref, table, load_sem.at[1])
    load_table.start()
    load_core = pltpu.make_async_copy(core_ref, core, load_sem.at[2])
    load_core.start()

    def radial_peer(jump):
        return (lax.rem(slab + jump, slabs), wedge)

    def phi_peer(jump):
        return (slab, lax.rem(wedge + jump, wedges))

    barrier = pltpu.get_barrier_semaphore()
    jumps = [(i, 0) for i in range(1, slabs)] + [(0, j) for j in range(1, wedges)]

    def peer_at(jump):
        return (radial_peer(jump[0])[0], phi_peer(jump[1])[1])

    for jump in jumps:
        pl.semaphore_signal(barrier, inc=1, device_id=peer_at(jump), device_id_type=MESH)
    load.wait()
    load_table.wait()
    load_core.wait()

    def remote(src, dst, send, recv, peer):
        return pltpu.make_async_remote_copy(
            src_ref=src, dst_ref=dst, send_sem=send, recv_sem=recv, device_id=peer,
            device_id_type=MESH,
        )

    def radial_copies(buffer, section, tile):
        where = pl.ds(PAD + TILE * tile, TILE)
        slot = (section * tiles + tile) * 2
        up = remote(
            buffer.at[:, pl.ds(rows, 2), where, :], buffer.at[:, pl.ds(0, 2), where, :],
            radial_send.at[slot], radial_recv.at[slot], radial_peer(1),
        )
        down = remote(
            buffer.at[:, pl.ds(2, 2), where, :], buffer.at[:, pl.ds(rows + 2, 2), where, :],
            radial_send.at[slot + 1], radial_recv.at[slot + 1], radial_peer(slabs - 1),
        )
        return up, down

    def radial_start(copies):
        up, down = copies

        @pl.when(has_up)
        def _():
            up.start()

        @pl.when(has_down)
        def _():
            down.start()

    def radial_sent(copies):
        up, down = copies

        @pl.when(has_up)
        def _():
            up.wait_send()

        @pl.when(has_down)
        def _():
            down.wait_send()

    def radial_land(copies, buffer, tile):
        up, down = copies
        where = pl.ds(PAD + TILE * tile, TILE)

        @pl.when(has_down)
        def _():
            up.wait_recv()

        @pl.when(jnp.logical_not(has_down))
        def _():
            value = buffer[:, 2, where, :]
            buffer[:, 0, where, :] = value
            buffer[:, 1, where, :] = value

        @pl.when(has_up)
        def _():
            down.wait_recv()

        @pl.when(jnp.logical_not(has_up))
        def _():
            value = buffer[:, rows + 1, where, :]
            buffer[:, rows + 2, where, :] = value
            buffer[:, rows + 3, where, :] = value

    whole, inside, low_edge, high_edge = (0, rows), (2, rows - 4), (0, 2), (rows - 2, 2)

    def phi_copies(section, piece, slot):
        where = pl.ds(*piece)
        return [
            remote(
                edge.at[section * 2 + side, :, where], halo.at[section * 2 + side, :, where],
                phi_send.at[slot + side], phi_recv.at[slot + side], phi_peer(jump),
            )
            for side, jump in ((0, wedges - 1), (1, 1))
        ]

    def phi_pack(buffer, section, side, piece):
        begin, count = piece
        start = PAD if side == 0 else PAD + cells - 2
        edge[section * 2 + side, :, pl.ds(begin, count)] = buffer[
            :, pl.ds(2 + begin, count), pl.ds(start, 2), :
        ]

    def phi_unpack(buffer, section, side, piece):
        begin, count = piece
        start = PAD + cells if side == 0 else PAD - 2
        buffer[:, pl.ds(2 + begin, count), pl.ds(start, 2), :] = halo[
            section * 2 + side, :, pl.ds(begin, count)
        ]

    shape = (TILE, lanes)
    lane = lax.broadcasted_iota(jnp.int32, (rows, lanes), 1)
    line = lax.broadcasted_iota(jnp.int32, (rows, lanes), 0)
    column = jnp.sum(first[0, pl.ds(2, rows), pl.ds(PAD, cells), :], axis=1)
    column = jnp.sum(column * table[0:1, :], axis=1, keepdims=True)
    centres = INNER_RADIUS + (
        (slab * rows + line).astype(jnp.float32) + 0.5
    ) * radial_step
    column = column * centres * centres * (radial_step * theta_step * phi_step)
    part[...] = jnp.sum(jnp.where(lane == line, column, 0.0), axis=0, keepdims=True)
    got[0] = part[...]
    phi_pack(first, 0, 0, whole)
    phi_pack(first, 0, 1, whole)
    pl.semaphore_wait(barrier, len(jumps))

    def wedge_sum():
        shells = jnp.zeros((1, lanes), jnp.float32)
        for w in range(wedges):
            shells = shells + got[lax.rem(wedge + wedges - w, wedges)]
        return shells

    part_copies = []
    for j in range(1, wedges):
        i, slot = 0, j
        part_copies.append(
            remote(part, got.at[slot], part_send.at[slot], part_recv.at[slot], peer_at((i, j)))
        )
    first_radial = [radial_copies(first, 0, t) for t in range(tiles)]
    second_radial = [radial_copies(second, 1, t) for t in range(tiles)]
    first_phi = phi_copies(0, whole, 0)
    inside_phi = phi_copies(1, inside, 2)
    low_phi, high_phi = phi_copies(1, low_edge, 4), phi_copies(1, high_edge, 6)
    for copy in part_copies + first_phi:
        copy.start()
    radial_start(first_radial[0])
    for copy in part_copies:
        copy.wait_recv()
    slab_part[...] = wedge_sum()
    slab_copies = []
    for j in range(1, slabs):
        slot = j * wedges
        slab_copies.append(
            remote(
                slab_part, got.at[slot], part_send.at[slot], part_recv.at[slot], radial_peer(j)
            )
        )
    for copy in slab_copies:
        copy.start()
    for t in range(1, tiles):
        radial_start(first_radial[t])

    lane_tile = lax.broadcasted_iota(jnp.int32, shape, 1)
    is_first, is_last = lane_tile == 0, lane_tile == lanes - 1

    def rate(buffer, r, tile, radial=True, rest=True):
        start = PAD + TILE * tile

        def at(row, offset):
            return [buffer[k, row + 2, pl.ds(start + offset, TILE), :] for k in range(variables)]

        def spread(value):
            return jnp.broadcast_to(value, shape)

        index = jnp.full(shape, slab * rows + r, jnp.int32).astype(jnp.float32)
        radius = INNER_RADIUS + (index + 0.5) * radial_step
        inner, outer = radius - 0.5 * radial_step, radius + 0.5 * radial_step
        inverse_r = 1.0 / radius
        centre = at(r, 0)
        total = [0.0] * variables
        if radial:
            lower, upper = two_faces([at(r + o, 0) if o else centre for o in range(-2, 3)], 1)
            scale = inverse_r * inverse_r * (1.0 / radial_step)
            area_in, area_out = inner * inner * scale, outer * outer * scale
            total = [area_in * a - area_out * b for a, b in zip(lower, upper)]
        if not rest:
            return total
        lower, upper = two_faces([at(r, o) if o else centre for o in range(-2, 3)], 3)
        around = inverse_r * spread(table[4:5, :])
        scale = around * (1.0 / phi_step)
        total = [t + (a - b) * scale for t, a, b in zip(total, lower, upper)]
        left, right = [], []
        for q in centre:
            after = jnp.where(is_last, q, pltpu.roll(q, lanes - 1, 1))
            above = after - q
            below = jnp.where(is_first, 0.0, pltpu.roll(above, 1, 1))
            slope = half_slope(below, above)
            left.append(q + slope)
            right.append(jnp.where(is_last, q, pltpu.roll(q - slope, lanes - 1, 1)))
        upper = flux(left, right, 2)
        scale = around * (1.0 / theta_step)
        low_sine, high_sine = spread(table[1:2, :]), spread(table[2:3, :])
        low_area, high_area = low_sine * scale, high_sine * scale
        total = [
            t + (low_area * pltpu.roll(f, 1, 1) - high_area * f) for t, f in zip(total, upper)
        ]
        density, inverse, pressure = thermo(centre)
        vr, vt, vp = (centre[m] * inverse for m in (1, 2, 3))
        cot = spread(table[3:4, :])
        total[1] = total[1] + (2.0 * pressure + density * (vt * vt + vp * vp)) * inverse_r
        total[2] = total[2] + (
            (pressure + density * vp * vp) * cot - density * vr * vt
        ) * inverse_r
        total[3] = total[3] - density * vp * (vr + vt * cot) * inverse_r
        return centre, density, total

    def gravity_at(r):
        return jnp.broadcast_to(pull[pl.ds(r, 1), :], shape)

    def with_gravity(rates, r):
        centre, density, total = rates
        gravity = gravity_at(r)
        total[1] = total[1] - density * gravity
        total[4] = total[4] - centre[1] * gravity
        return centre, total

    def section_one(r, tile):
        centre, _, total = rate(first, r, tile)
        where = pl.ds(PAD + TILE * tile, TILE)
        for k in range(variables):
            second[k, r + 2, where, :] = centre[k] + timestep * total[k]

    def rest_one(r, tile):
        centre, _, total = rate(first, r, tile, radial=False)
        where = pl.ds(PAD + TILE * tile, TILE)
        for k in range(variables):
            second[k, r + 2, where, :] = centre[k] + timestep * total[k]

    def radial_one(r, tile):
        total = rate(first, r, tile, rest=False)
        where = pl.ds(PAD + TILE * tile, TILE)
        for k in range(variables):
            second[k, r + 2, where, :] = second[k, r + 2, where, :] + timestep * total[k]

    def late_gravity(r, tile):
        where = pl.ds(PAD + TILE * tile, TILE)
        gravity = timestep * gravity_at(r)
        density = jnp.maximum(first[0, r + 2, where, :], MINIMUM_DENSITY)
        second[1, r + 2, where, :] = second[1, r + 2, where, :] - density * gravity
        second[4, r + 2, where, :] = (
            second[4, r + 2, where, :] - first[1, r + 2, where, :] * gravity
        )

    def section_two(r, tile, radial=True):
        centre, total = with_gravity(rate(second, r, tile, radial=radial), r)
        where = pl.ds(PAD + TILE * tile, TILE)
        into = pl.ds(TILE * tile, TILE)
        for k in range(variables):
            begin = first[k, r + 2, where, :]
            out_ref[k, r, into, :] = 0.5 * begin + 0.5 * (centre[k] + timestep * total[k])

    def radial_two(r, tile):
        total = rate(second, r, tile, rest=False)
        into = pl.ds(TILE * tile, TILE)
        for k in range(variables):
            out_ref[k, r, into, :] = out_ref[k, r, into, :] + (0.5 * timestep) * total[k]

    def each_row(low, high, step):
        lax.fori_loop(low, high, lambda r, _: (step(r), 0)[1], 0)

    def each_edge(step):
        lax.fori_loop(
            0, 4, lambda i, _: (step(i + (i // 2) * (rows - 4)), 0)[1], 0
        )

    def all_tiles(step):
        def run(r):
            for t in range(tiles):
                step(r, t)

        return run

    for side, copy in enumerate(first_phi):
        copy.wait_recv()
        phi_unpack(first, 0, side, whole)
    each_row(2, rows - 2, all_tiles(section_one))
    each_edge(all_tiles(rest_one))
    radial_land(first_radial[0], first, 0)
    each_edge(lambda r: radial_one(r, 0))

    for copy in slab_copies:
        copy.wait_recv()
    before = jnp.zeros((1, lanes), jnp.float32)
    for j in range(slabs - 1, 0, -1):
        before = before + jnp.where(slab >= j, got[j * wedges], 0.0)
    before = jnp.sum(before, axis=1, keepdims=True)
    weight = jnp.where(lane < line, 1.0, jnp.where(lane == line, 0.5, 0.0))
    within = jnp.sum(weight * slab_part[...], axis=1, keepdims=True)
    enclosed = core[0] + before + within + jnp.zeros((rows, lanes), jnp.float32)
    mass_ref[...] = jnp.sum(jnp.where(lane == line, enclosed, 0.0), axis=0, keepdims=True)[:, :rows]
    pull[...] = strength * enclosed / (centres * centres)
    for t in range(tiles):
        if t:
            radial_land(first_radial[t], first, t)
            each_edge(lambda r: radial_one(r, t))
        each_edge(lambda r: late_gravity(r, t))
        radial_start(second_radial[t])
        for side, last in ((0, 0), (1, tiles - 1)):
            if t == last:
                phi_pack(second, 1, side, low_edge)
                phi_pack(second, 1, side, high_edge)
                low_phi[side].start()
                high_phi[side].start()
        if t == 0:
            each_row(2, rows - 2, all_tiles(late_gravity))
            for side, copy in enumerate(inside_phi):
                phi_pack(second, 1, side, inside)
                copy.start()
    for side, copy in enumerate(inside_phi):
        copy.wait_recv()
        phi_unpack(second, 1, side, inside)
    each_row(2, rows - 2, all_tiles(section_two))
    for side in range(2):
        low_phi[side].wait_recv()
        high_phi[side].wait_recv()
        phi_unpack(second, 1, side, low_edge)
        phi_unpack(second, 1, side, high_edge)
    each_edge(all_tiles(lambda r, t: section_two(r, t, False)))
    for t in range(tiles):
        radial_land(second_radial[t], second, t)
        each_edge(lambda r: radial_two(r, t))

    for copy in part_copies + slab_copies + first_phi + inside_phi + low_phi + high_phi:
        copy.wait_send()
    for copies in first_radial + second_radial:
        radial_sent(copies)


def body(conserved, core_mass):
    variables, rows, cells, lanes = conserved.shape
    slabs, wedges = lax.axis_size("radial"), lax.axis_size("phi")
    sizes = step_sizes(rows * slabs, cells * wedges, lanes)
    table = jnp.asarray(angle_tables(lanes, sizes[1]))
    tiles = cells // TILE
    padded = (variables, rows + 4, cells + 2 * PAD, lanes)
    vmem = pl.BlockSpec(memory_space=pltpu.VMEM)
    dma = pltpu.SemaphoreType.DMA
    advanced, mass = pl.pallas_call(
        functools.partial(kernel, sizes, (slabs, wedges)),
        out_shape=(
            pltpu.VMEM(conserved.shape, jnp.float32),
            pltpu.VMEM((1, rows), jnp.float32),
        ),
        in_specs=[pl.BlockSpec(memory_space=pl.ANY)] * 3,
        out_specs=(vmem, vmem),
        scratch_shapes=[
            pltpu.VMEM(padded, jnp.float32),
            pltpu.VMEM(padded, jnp.float32),
            pltpu.VMEM((4, variables, rows, 2, lanes), jnp.float32),
            pltpu.VMEM((4, variables, rows, 2, lanes), jnp.float32),
            pltpu.VMEM((1, lanes), jnp.float32),
            pltpu.VMEM((1, lanes), jnp.float32),
            pltpu.VMEM((slabs * wedges, 1, lanes), jnp.float32),
            pltpu.VMEM((rows, lanes), jnp.float32),
            pltpu.VMEM((TILE, lanes), jnp.float32),
            pltpu.SMEM((1,), jnp.float32),
            dma((3,)),
            dma((4 * tiles,)),
            dma((4 * tiles,)),
            dma((8,)),
            dma((8,)),
            dma((slabs * wedges,)),
            dma((slabs * wedges,)),
        ],
        compiler_params=pltpu.CompilerParams(collective_id=0, has_side_effects=True),
    )(core_mass, table, conserved)
    return advanced, mass.reshape(rows)


def solution(mesh):
    in_specs = (P(None, "radial", "phi", None), P())
    out_specs = (P(None, "radial", "phi", None), P("radial"))
    return jax.shard_map(body, mesh=mesh, in_specs=in_specs, out_specs=out_specs, check_vma=False)
```

profile of v0, /device:TPU:1, one launch (start us, length us, event | category | flops | bytes accessed | tf_op | source)
XLA Modules:
  0.0 34.1 jit_solution(6911769714223704333)
XLA Ops:
  1.3 31.5 %shard_map.50 = (f32[8,8,16,128]{3,2,1,0:T(8,128)S(1)}, f32[1,8]{1,0:T(1,128)S(1)}) custom-call(f32[1]{0:T(128)S(6)} %copy.9.core_ref, f32[8,128]{1,0:T(8,128)} %constant.2.clone.table_ref, f32[8,8,16,128]{3,2,1,0:T(8,128)} %input_ref.1), custom_call_target="tpu_custom_call" | custom-call | tf_op jit(solution)/shard_map/pallas_call | solution.py:478
  32.8 0.8 %copy.7 = f32[8,8,16,128]{3,2,1,0:T(8,128)} copy(f32[8,8,16,128]{3,2,1,0:T(8,128)S(1)} %get-tuple-element.6) | data formatting | bytes 1048576
  33.5 0.5 %copy.8 = f32[8]{0:T(128)} copy(f32[8]{0:T(128)S(1)} %bitcast.1) | data formatting | bytes 64
where the time goes:
time: 34.2 us; the launch traced here: 34.1 us
  Pallas kernels  31.5 us (92%)
  local copies, waits for them, and re-layouts  1.31 us (4%)
  between operations  1.28 us (4%)
    pallas_call x1, Pallas kernels, body(): pl.pallas_call(functools.partial(kernel, sizes, (slabs, wedges)), out_sha...  31.5 us
    unnamed x2, local copies, waits for them, and re-layouts  1.31 us

commit v1 on v0

v1 whole, which is shorter than its diff:
```python
import functools
import math

import jax
import jax.numpy as jnp
import numpy as np
from jax import lax
from jax.experimental import pallas as pl
from jax.experimental.pallas import tpu as pltpu
from jax.sharding import PartitionSpec as P

ADIABATIC = 4.0 / 3.0
INNER_RADIUS = 1.0
OUTER_RADIUS = 2.0
COURANT = 0.4
GRAVITY_KICK = 0.004
MINIMUM_DENSITY = 0.05
PRESSURE_FLOOR = 0.01
MESH = pl.DeviceIdType.MESH
TILE = 8
PAD = 8


def step_sizes(radial_total, phi_total, theta_total):
    theta_step = math.pi / theta_total
    phi_step = 2.0 * math.pi / phi_total
    polar_width = INNER_RADIUS * math.sin(0.5 * theta_step) * phi_step
    radial_step = min(2.0 * polar_width, (OUTER_RADIUS - INNER_RADIUS) / radial_total)
    timestep = COURANT * min(radial_step, polar_width)
    return (radial_step, theta_step, phi_step, timestep)


def angle_tables(theta_cells, theta_step):
    step = np.float32(theta_step)
    centre = (np.arange(theta_cells, dtype=np.float32) + np.float32(0.5)) * step
    face = np.arange(theta_cells + 1, dtype=np.float32) * step
    sine = np.sin(centre.astype(np.float64))
    cosine = np.cos(centre.astype(np.float64))
    face_sine = np.sin(face.astype(np.float64))
    face_sine[-1] = 0.0
    zero = np.zeros(theta_cells)
    upper = 0.5 * face_sine[1:] / theta_step
    rows = [sine, upper, cosine / sine, 1.0 / sine, zero, zero, zero, zero]
    return np.stack(rows).astype(np.float32)


def half_slope(below, above):
    high, low = jnp.maximum(below, 0.0), jnp.minimum(below, 0.0)
    return 0.5 * jnp.maximum(jnp.minimum(above, high), low)


def thermo(q):
    density = jnp.maximum(q[0], MINIMUM_DENSITY)
    inverse = 1.0 / density
    kinetic = 0.5 * (q[1] * q[1] + q[2] * q[2] + q[3] * q[3]) * inverse
    pressure = jnp.maximum((ADIABATIC - 1.0) * (q[4] - kinetic), PRESSURE_FLOOR * density)
    return density, inverse, pressure


def physical(q, component):
    _, inverse, pressure = thermo(q)
    normal = q[component] * inverse
    squared = ADIABATIC * pressure * inverse
    return normal, pressure, jnp.abs(normal) + squared * lax.rsqrt(squared)


def flux(left, right, component, half_area):
    left_v, left_p, left_a = physical(left, component)
    right_v, right_p, right_a = physical(right, component)
    signal = jnp.maximum(left_a, right_a)
    left_w = half_area * (left_v + signal)
    right_w = half_area * (right_v - signal)
    out = [a * left_w + b * right_w for a, b in zip(left, right)]
    out[component] = out[component] + half_area * (left_p + right_p)
    out[4] = out[4] + half_area * (left_p * left_v + right_p * right_v)
    return out


def kernel(
    sizes,
    counts,
    core_ref,
    table_ref,
    input_ref,
    out_ref,
    mass_ref,
    first,
    second,
    edge,
    halo,
    radial,
    ends,
    part,
    slab_part,
    got_part,
    got,
    got_above,
    pull,
    table,
    core,
    load_sem,
    radial_send,
    radial_recv,
    phi_send,
    phi_recv,
    part_send,
    part_recv,
    slab_send,
    slab_recv,
    above_send,
    above_recv,
):
    radial_step, theta_step, phi_step, timestep = sizes
    slabs, wedges = counts
    variables, rows, cells, lanes = input_ref.shape
    tiles = cells // TILE
    strength = GRAVITY_KICK / timestep
    slab, wedge = lax.axis_index("radial"), lax.axis_index("phi")
    has_up, has_down = slab < slabs - 1, slab > 0
    shape = (TILE, lanes)

    load = pltpu.make_async_copy(
        input_ref, first.at[:, pl.ds(2, rows), pl.ds(PAD, cells), :], load_sem.at[0]
    )
    load.start()
    load_table = pltpu.make_async_copy(table_ref, table, load_sem.at[1])
    load_table.start()
    load_core = pltpu.make_async_copy(core_ref, core, load_sem.at[2])
    load_core.start()

    def radial_peer(jump):
        return (slab + jump, wedge)

    def phi_peer(jump):
        return (slab, lax.rem(wedge + jump, wedges))

    barrier = pltpu.get_barrier_semaphore()

    def greet(peer):
        pl.semaphore_signal(barrier, inc=1, device_id=peer, device_id_type=MESH)

    for j in range(1, wedges):
        greet(phi_peer(j))

    @pl.when(has_up)
    def _():
        greet(radial_peer(1))

    lax.fori_loop(1, slab + 1, lambda j, _: (greet(radial_peer(-j)), 0)[1], 0)
    greeted = (wedges - 1) + (slabs - 1 - slab) + jnp.where(has_down, 1, 0)

    load.wait()
    load_table.wait()
    load_core.wait()

    def remote(src, dst, send, recv, peer):
        return pltpu.make_async_remote_copy(
            src_ref=src, dst_ref=dst, send_sem=send, recv_sem=recv, device_id=peer,
            device_id_type=MESH,
        )

    def radial_copies(buffer, section):
        where, slot = pl.ds(PAD, cells), 2 * section
        up = remote(
            buffer.at[:, pl.ds(rows, 2), where, :], buffer.at[:, pl.ds(0, 2), where, :],
            radial_send.at[slot], radial_recv.at[slot], radial_peer(1),
        )
        down = remote(
            buffer.at[:, pl.ds(2, 2), where, :], buffer.at[:, pl.ds(rows + 2, 2), where, :],
            radial_send.at[slot + 1], radial_recv.at[slot + 1], radial_peer(-1),
        )
        return up, down

    def radial_start(copies):
        up, down = copies
        pl.when(has_up)(up.start)
        pl.when(has_down)(down.start)

    def radial_sent(copies):
        up, down = copies
        pl.when(has_up)(up.wait_send)
        pl.when(has_down)(down.wait_send)

    def radial_land(copies):
        up, down = copies
        pl.when(has_down)(up.wait_recv)
        pl.when(has_up)(down.wait_recv)

    def radial_ends(buffer):
        for t in range(tiles):
            where = pl.ds(PAD + TILE * t, TILE)

            @pl.when(jnp.logical_not(has_down))
            def _():
                value = buffer[:, 2, where, :]
                buffer[:, 0, where, :] = value
                buffer[:, 1, where, :] = value

            @pl.when(jnp.logical_not(has_up))
            def _():
                value = buffer[:, rows + 1, where, :]
                buffer[:, rows + 2, where, :] = value
                buffer[:, rows + 3, where, :] = value

    def phi_copies(section):
        slot = 2 * section
        return [
            remote(
                edge.at[slot + side], halo.at[slot + side],
                phi_send.at[slot + side], phi_recv.at[slot + side], phi_peer(jump),
            )
            for side, jump in ((0, wedges - 1), (1, 1))
        ]

    def phi_pack(buffer, section):
        for side, start in ((0, PAD), (1, PAD + cells - 2)):
            edge[section * 2 + side] = buffer[:, pl.ds(2, rows), pl.ds(start, 2), :]

    def phi_unpack(buffer, section):
        for side, start in ((0, PAD + cells), (1, PAD - 2)):
            buffer[:, pl.ds(2, rows), pl.ds(start, 2), :] = halo[section * 2 + side]

    lane = lax.broadcasted_iota(jnp.int32, (rows, lanes), 1)
    line = lax.broadcasted_iota(jnp.int32, (rows, lanes), 0)
    column = jnp.sum(first[0, pl.ds(2, rows), pl.ds(PAD, cells), :], axis=1)
    column = jnp.sum(column * table[0:1, :], axis=1, keepdims=True)
    centres = INNER_RADIUS + (
        (slab * rows + line).astype(jnp.float32) + 0.5
    ) * radial_step
    column = column * centres * centres * (radial_step * theta_step * phi_step)
    part[...] = jnp.sum(jnp.where(lane == line, column, 0.0), axis=0, keepdims=True)
    phi_pack(first, 0)

    sub = lax.broadcasted_iota(jnp.int32, shape, 0)
    lane_tile = lax.broadcasted_iota(jnp.int32, shape, 1)
    is_last = lane_tile == lanes - 1
    is_top, is_bottom = sub == TILE - 1, sub == 0

    def spread(value):
        return jnp.broadcast_to(value, shape)

    def radius_of(index):
        index = jnp.full(shape, slab * rows + index, jnp.int32).astype(jnp.float32)
        return INNER_RADIUS + (index + 0.5) * radial_step

    def radial_faces(buffer, low, count, tile):
        where = pl.ds(PAD + TILE * tile, TILE)
        lefts = [[] for _ in range(count)]
        rights = [[] for _ in range(count)]
        for k in range(variables):
            q = [buffer[k, low + j, where, :] for j in range(count + 3)]
            step = [q[j + 1] - q[j] for j in range(count + 2)]
            slope = [half_slope(step[j], step[j + 1]) for j in range(count + 1)]
            for i in range(count):
                lefts[i].append(q[i + 1] + slope[i])
                rights[i].append(q[i + 2] - slope[i + 1])
        out = []
        for i in range(count):
            face = radius_of(low + i) - 0.5 * radial_step
            out.append(flux(lefts[i], rights[i], 1, face * face * (0.5 / radial_step)))
        return out

    def radial_store(buffer, low, count):
        for t in range(tiles):
            for i, face in enumerate(radial_faces(buffer, low, count, t)):
                for k in range(variables):
                    radial[k, low + i, pl.ds(TILE * t, TILE), :] = face[k]

    def theta_part(centre):
        left, right = [], []
        for q in centre:
            after = pltpu.roll(q, lanes - 1, 1)
            above = jnp.where(is_last, 0.0, after - q)
            below = pltpu.roll(above, 1, 1)
            slope = half_slope(below, above)
            left.append(q + slope)
            right.append(pltpu.roll(q - slope, lanes - 1, 1))
        upper = flux(left, right, 2, spread(table[1:2, :]))
        return [pltpu.roll(f, 1, 1) - f for f in upper]

    def phi_ends(buffer):
        def column_at(k, cell):
            return buffer[k, pl.ds(2, rows), PAD + cell, :]

        left, right = [], []
        for k in range(variables):
            a, b, c, d = (column_at(k, cell) for cell in (-2, -1, 0, 1))
            left.append(b + half_slope(b - a, c - b))
            right.append(c - half_slope(c - b, d - c))
            a, b, c = (column_at(k, cell) for cell in (cells - 1, cells, cells + 1))
            ends[1, k] = b - half_slope(b - a, c - b)
        for k, f in enumerate(flux(left, right, 3, 0.5 / phi_step)):
            ends[0, k] = f

    def phi_part(buffer, r):
        left, right = [[] for _ in range(tiles)], [[] for _ in range(tiles)]
        for k in range(variables):
            turned = []
            for t in range(tiles):
                start = PAD + TILE * t
                a, b, c = (
                    buffer[k, r + 2, pl.ds(start + offset, TILE), :] for offset in (-1, 0, 1)
                )
                slope = half_slope(b - a, c - b)
                left[t].append(b + slope)
                turned.append(pltpu.roll(b - slope, TILE - 1, 0))
            turned.append(spread(ends[1, k, pl.ds(r, 1), :]))
            for t in range(tiles):
                right[t].append(jnp.where(is_top, turned[t + 1], turned[t]))
        upper = [flux(left[t], right[t], 3, 0.5 / phi_step) for t in range(tiles)]
        out = [[] for _ in range(tiles)]
        for k in range(variables):
            before = spread(ends[0, k, pl.ds(r, 1), :])
            for t in range(tiles):
                turned = pltpu.roll(upper[t][k], 1, 0)
                out[t].append(jnp.where(is_bottom, before, turned) - upper[t][k])
                before = turned
        return out

    def sources(centre, inverse_r):
        density, inverse, pressure = thermo(centre)
        vr, vt, vp = (centre[m] * inverse for m in (1, 2, 3))
        cot = spread(table[2:3, :])
        swirl = density * vp * vp
        return density, [
            (2.0 * pressure + density * vt * vt + swirl) * inverse_r,
            ((pressure + swirl) * cot - density * vr * vt) * inverse_r,
            -density * vp * (vr + vt * cot) * inverse_r,
        ]

    def centre_at(buffer, r, tile):
        return [
            buffer[k, r + 2, pl.ds(PAD + TILE * tile, TILE), :] for k in range(variables)
        ]

    def early_one(r):
        inverse_r = 1.0 / radius_of(r)
        around = inverse_r * spread(table[3:4, :]) * timestep
        for t in range(tiles):
            centre = centre_at(first, r, t)
            total = [c + d * around for c, d in zip(centre, theta_part(centre))]
            _, source = sources(centre, inverse_r)
            for m in range(3):
                total[m + 1] = total[m + 1] + timestep * source[m]
            for k in range(variables):
                second[k, r + 2, pl.ds(PAD + TILE * t, TILE), :] = total[k]

    def late_one(r):
        inverse_r = 1.0 / radius_of(r)
        around = inverse_r * spread(table[3:4, :]) * timestep
        along = inverse_r * inverse_r * timestep
        for t, part_of in enumerate(phi_part(first, r)):
            into = pl.ds(TILE * t, TILE)
            where = pl.ds(PAD + TILE * t, TILE)
            for k in range(variables):
                across = radial[k, r, into, :] - radial[k, r + 1, into, :]
                second[k, r + 2, where, :] = (
                    second[k, r + 2, where, :] + part_of[k] * around + across * along
                )

    def section_two(r):
        inverse_r = 1.0 / radius_of(r)
        scale = 0.5 * timestep
        around = inverse_r * spread(table[3:4, :]) * scale
        along = inverse_r * inverse_r * scale
        gravity = spread(pull[pl.ds(r + 8, 1), :])
        phi = phi_part(second, r)
        for t in range(tiles):
            into = pl.ds(TILE * t, TILE)
            where = pl.ds(PAD + TILE * t, TILE)
            upper = radial_faces(second, r + 1, 1, t)[0]
            lower = [radial[k, r, into, :] for k in range(variables)]
            for k in range(variables):
                radial[k, r + 1, into, :] = upper[k]
            centre = centre_at(second, r, t)
            theta = theta_part(centre)
            density, source = sources(centre, inverse_r)
            source[0] = source[0] - density * gravity
            source.append(-centre[1] * gravity)
            total = [
                0.5 * (first[k, r + 2, where, :] + centre[k])
                + (theta[k] + phi[t][k]) * around
                + (lower[k] - upper[k]) * along
                for k in range(variables)
            ]
            for m in range(4):
                total[m + 1] = total[m + 1] + scale * source[m]
            for k in range(variables):
                out_ref[k, r, into, :] = total[k]

    def each(low, high, step):
        lax.fori_loop(low, high, lambda r, _: (step(r), 0)[1], 0)

    def each_pair(low, high, step):
        def both(i):
            step(2 * i)
            step(2 * i + 1)

        each(low // 2, high // 2, both)

    each_pair(0, rows, early_one)
    each(0, 2, lambda i: radial_store(first, 2 + 2 * i, 2))
    radial_store(first, 6, 1)

    pl.semaphore_wait(barrier, greeted)

    part_copies = [
        remote(part, got_part.at[j], part_send.at[j], part_recv.at[j], phi_peer(j))
        for j in range(1, wedges)
    ]
    first_radial, second_radial = radial_copies(first, 0), radial_copies(second, 1)
    first_phi, second_phi = phi_copies(0), phi_copies(1)
    for copy in part_copies:
        copy.start()
    radial_start(first_radial)
    for copy in first_phi:
        copy.start()
    got_part[0] = part[...]
    for copy in part_copies:
        copy.wait_recv()
    shells = jnp.zeros((1, lanes), jnp.float32)
    for w in range(wedges):
        shells = shells + got_part[lax.rem(wedge + wedges - w, wedges)]
    slab_part[...] = shells

    def slab_copy(j):
        return remote(
            slab_part, got.at[j], slab_send.at[j], slab_recv.at[j], radial_peer(j)
        )

    above_copy = remote(
        slab_part, got_above, above_send.at[0], above_recv.at[0], radial_peer(-1)
    )
    each(1, slabs - slab, lambda j: slab_copy(j).start())
    pl.when(has_down)(above_copy.start)

    for copy in first_phi:
        copy.wait_recv()
    phi_unpack(first, 0)
    radial_land(first_radial)
    radial_ends(first)
    phi_ends(first)
    each(0, 2, lambda i: radial_store(first, 7 * i, 2))
    each(0, rows, late_one)
    phi_pack(second, 1)
    radial_start(second_radial)
    for copy in second_phi:
        copy.start()

    after = jnp.where(lane < line, 1.0, jnp.where(lane == line, 0.5, 0.0))
    within = jnp.sum(after * slab_part[...], axis=1, keepdims=True)
    whole = jnp.sum(jnp.where(line >= 0, slab_part[...], 0.0), axis=1, keepdims=True)

    for copy in second_phi:
        copy.wait_recv()
    phi_unpack(second, 1)
    radial_land(second_radial)

    radial_sent(second_radial)
    pl.when(has_up)(above_copy.wait_recv)
    each(1, slab + 1, lambda j: slab_copy(j).wait_recv())
    sums = [jnp.zeros((1, lanes), jnp.float32) for _ in range(4)]
    for j in range(1, slabs):
        sums[j % 4] = sums[j % 4] + jnp.where(slab >= j, got[j], 0.0)
    before = jnp.broadcast_to((sums[0] + sums[1]) + (sums[2] + sums[3]), (rows, lanes))
    before = core[0] + jnp.sum(before, axis=1, keepdims=True)
    inner = jnp.where(lane > line, 1.0, jnp.where(lane == line, 0.5, 0.0))
    inner = jnp.sum(inner * got[1], axis=1, keepdims=True)
    outer = jnp.sum(after * got_above[...], axis=1, keepdims=True)
    wide = jnp.zeros((rows, lanes), jnp.float32)
    enclosed = before + within + wide
    mass_ref[...] = jnp.sum(jnp.where(lane == line, enclosed, 0.0), axis=0, keepdims=True)[:, :rows]
    for i, inside in ((0, before - inner), (1, before + within), (2, before + whole + outer)):
        at = centres + (i - 1) * rows * radial_step
        pull[pl.ds(8 * i, 8), :] = strength * (inside + wide) / (at * at)

    def pulled(row, start):
        where = pl.ds(start, TILE)
        gravity = timestep * spread(pull[pl.ds(row + 6, 1), :])
        density = jnp.maximum(first[0, row, where, :], MINIMUM_DENSITY)
        second[1, row, where, :] = second[1, row, where, :] - density * gravity
        second[4, row, where, :] = second[4, row, where, :] - first[1, row, where, :] * gravity

    def pulled_row(row):
        for t in range(-1, tiles + 1):
            pulled(row, PAD + TILE * t)

    each_pair(0, rows + 4, pulled_row)
    radial_ends(second)

    phi_ends(second)
    radial_store(second, 0, 1)
    each(0, rows, section_two)

    for copy in part_copies + first_phi + second_phi:
        copy.wait_send()
    radial_sent(first_radial)
    each(1, slabs - slab, lambda j: slab_copy(j).wait_send())
    pl.when(has_down)(above_copy.wait_send)


def body(conserved, core_mass):
    variables, rows, cells, lanes = conserved.shape
    slabs, wedges = lax.axis_size("radial"), lax.axis_size("phi")
    sizes = step_sizes(rows * slabs, cells * wedges, lanes)
    table = jnp.asarray(angle_tables(lanes, sizes[1]))
    padded = (variables, rows + 4, cells + 2 * PAD, lanes)
    vmem = pl.BlockSpec(memory_space=pltpu.VMEM)
    dma = pltpu.SemaphoreType.DMA
    advanced, mass = pl.pallas_call(
        functools.partial(kernel, sizes, (slabs, wedges)),
        out_shape=(
            pltpu.VMEM(conserved.shape, jnp.float32),
            pltpu.VMEM((1, rows), jnp.float32),
        ),
        in_specs=[pl.BlockSpec(memory_space=pl.ANY)] * 3,
        out_specs=(vmem, vmem),
        scratch_shapes=[
            pltpu.VMEM(padded, jnp.float32),
            pltpu.VMEM(padded, jnp.float32),
            pltpu.VMEM((4, variables, rows, 2, lanes), jnp.float32),
            pltpu.VMEM((4, variables, rows, 2, lanes), jnp.float32),
            pltpu.VMEM((variables, rows + 1, cells, lanes), jnp.float32),
            pltpu.VMEM((2, variables, rows, lanes), jnp.float32),
            pltpu.VMEM((1, lanes), jnp.float32),
            pltpu.VMEM((1, lanes), jnp.float32),
            pltpu.VMEM((wedges, 1, lanes), jnp.float32),
            pltpu.VMEM((slabs, 1, lanes), jnp.float32),
            pltpu.VMEM((1, lanes), jnp.float32),
            pltpu.VMEM((3 * TILE, lanes), jnp.float32),
            pltpu.VMEM((TILE, lanes), jnp.float32),
            pltpu.SMEM((1,), jnp.float32),
            dma((3,)),
            dma((4,)),
            dma((4,)),
            dma((4,)),
            dma((4,)),
            dma((wedges,)),
            dma((wedges,)),
            dma((slabs,)),
            dma((slabs,)),
            dma((1,)),
            dma((1,)),
        ],
        compiler_params=pltpu.CompilerParams(collective_id=0, has_side_effects=True),
    )(core_mass, table, conserved)
    return advanced, mass.reshape(rows)


def solution(mesh):
    in_specs = (P(None, "radial", "phi", None), P())
    out_specs = (P(None, "radial", "phi", None), P("radial"))
    return jax.shard_map(body, mesh=mesh, in_specs=in_specs, out_specs=out_specs, check_vma=False)
```

time: 34.2 us -> 30 us (0.88)
  Pallas kernels: 31.5 us -> 27.3 us
    pallas_call x1, Pallas kernels: 31.5 us -> 27.3 us  [body(): pl.pallas_call(functools.partial(kernel, sizes, (slabs, wedges)), out_sha...]
where the time goes in v1:
time: 30 us; the launch traced here: 29.9 us
  Pallas kernels  27.3 us (91%)
  local copies, waits for them, and re-layouts  1.31 us (4%)
  between operations  1.28 us (4%)
    pallas_call x1, Pallas kernels, body(): pl.pallas_call(functools.partial(kernel, sizes, (slabs, wedges)), out_sha...  27.3 us
    unnamed x2, local copies, waits for them, and re-layouts  1.31 us

profile of v1, /device:TPU:1, one launch (start us, length us, event | category | flops | bytes accessed | tf_op | source)
XLA Modules:
  0.0 29.9 jit_solution(10077173130959911461)
XLA Ops:
  1.3 27.3 %shard_map.50 = (f32[8,8,16,128]{3,2,1,0:T(8,128)S(1)}, f32[1,8]{1,0:T(1,128)S(1)}) custom-call(f32[1]{0:T(128)S(6)} %copy.9.core_ref, f32[8,128]{1,0:T(8,128)} %constant.2.clone.table_ref, f32[8,8,16,128]{3,2,1,0:T(8,128)} %input_ref.1), custom_call_target="tpu_custom_call" | custom-call | tf_op jit(solution)/shard_map/pallas_call | solution.py:510
  28.6 0.8 %copy.7 = f32[8,8,16,128]{3,2,1,0:T(8,128)} copy(f32[8,8,16,128]{3,2,1,0:T(8,128)S(1)} %get-tuple-element.6) | data formatting | bytes 1048576
  29.4 0.5 %copy.8 = f32[8]{0:T(128)} copy(f32[8]{0:T(128)S(1)} %bitcast.1) | data formatting | bytes 64

commit v2 on v1

--- a/solution.py
+++ b/solution.py
@@ -19,6 +19,9 @@
 MESH = pl.DeviceIdType.MESH
 TILE = 8
 PAD = 8
+DEPTH = 8
+LINE = 2 * DEPTH
+TOP = 4
 
 
 def step_sizes(radial_total, phi_total, theta_total):
@@ -98,6 +101,8 @@
     pull,
     table,
     core,
+    far,
+    turn,
     load_sem,
     radial_send,
     radial_recv,
@@ -107,7 +112,6 @@
     part_recv,
     slab_send,
     slab_recv,
-    above_send,
     above_recv,
 ):
     radial_step, theta_step, phi_step, timestep = sizes
@@ -134,20 +138,47 @@
     def phi_peer(jump):
         return (slab, lax.rem(wedge + jump, wedges))
 
+    def each(low, high, step):
+        lax.fori_loop(low, high, lambda r, _: (step(r), 0)[1], 0)
+
     barrier = pltpu.get_barrier_semaphore()
-
-    def greet(peer):
-        pl.semaphore_signal(barrier, inc=1, device_id=peer, device_id_type=MESH)
+    x, z, c = slab // LINE, (slab // 2) % DEPTH, slab % 2
+    level = jnp.where(z < TOP, z, TOP + x)
+    rank = jnp.where(z < TOP, 2 * x + c, 2 * (z - TOP) + c)
+    span, levels = slabs // DEPTH, DEPTH
+    turns = jnp.logical_and(slab % LINE == 0, has_down)
+    turned_to = jnp.logical_and(slab % LINE == LINE - 1, has_up)
+    plain_down = jnp.logical_and(has_down, jnp.logical_not(turns))
+
+    def signal(semaphore, peer):
+        pl.semaphore_signal(semaphore, inc=1, device_id=peer, device_id_type=MESH)
+
+    def each_slab(low, high, step):
+        def one_level(at):
+            for i in range(span):
+                spread_out = LINE * (i // 2) + 2 * at + i % 2
+                step(jnp.where(at < TOP, spread_out, LINE * (at - TOP) + LINE // 2 + i))
+
+        each(low, high, one_level)
+
+    def greet(v):
+        signal(barrier, (v, wedge))
+
+    def greet_level(v):
+        pl.when(jnp.logical_or(v < slab, v == slab + 1))(lambda: greet(v))
 
     for j in range(1, wedges):
-        greet(phi_peer(j))
-
-    @pl.when(has_up)
-    def _():
-        greet(radial_peer(1))
-
-    lax.fori_loop(1, slab + 1, lambda j, _: (greet(radial_peer(-j)), 0)[1], 0)
-    greeted = (wedges - 1) + (slabs - 1 - slab) + jnp.where(has_down, 1, 0)
+        signal(barrier, phi_peer(j))
+    pl.when(jnp.logical_and(z > 0, jnp.logical_and(z <= TOP, c == 0)))(lambda: greet(slab - 1))
+    each_slab(level, level + 1, greet_level)
+    each_slab(level + 1, levels, greet)
+    inside = jnp.where(z < TOP, 2 * c, jnp.where(rank > 0, 1, 0))
+    greeted = (wedges - 1) + span * level + (span - 1 - rank) + inside
+    further = slabs // LINE - 1 - x
+    heard = (
+        jnp.where(z < TOP, (TOP - 1 - z) * 2 * (further + 1), 0),
+        jnp.where(z < TOP, (DEPTH - TOP) * 2 * (further + 1), span * further),
+    )
 
     load.wait()
     load_table.wait()
@@ -163,18 +194,18 @@
         where, slot = pl.ds(PAD, cells), 2 * section
         up = remote(
             buffer.at[:, pl.ds(rows, 2), where, :], buffer.at[:, pl.ds(0, 2), where, :],
-            radial_send.at[slot], radial_recv.at[slot], radial_peer(1),
+            radial_send.at[0], radial_recv.at[slot], radial_peer(1),
         )
         down = remote(
             buffer.at[:, pl.ds(2, 2), where, :], buffer.at[:, pl.ds(rows + 2, 2), where, :],
-            radial_send.at[slot + 1], radial_recv.at[slot + 1], radial_peer(-1),
+            radial_send.at[1], radial_recv.at[slot + 1], radial_peer(-1),
         )
         return up, down
 
     def radial_start(copies):
         up, down = copies
         pl.when(has_up)(up.start)
-        pl.when(has_down)(down.start)
+        pl.when(plain_down)(down.start)
 
     def radial_sent(copies):
         up, down = copies
@@ -207,10 +238,17 @@
         return [
             remote(
                 edge.at[slot + side], halo.at[slot + side],
-                phi_send.at[slot + side], phi_recv.at[slot + side], phi_peer(jump),
+                phi_send.at[section], phi_recv.at[section], phi_peer(jump),
             )
             for side, jump in ((0, wedges - 1), (1, 1))
         ]
+
+    def phi_both(section):
+        slots = pl.ds(2 * section, 2)
+        return remote(
+            edge.at[slots], halo.at[slots], phi_send.at[section], phi_recv.at[section],
+            phi_peer(1),
+        )
 
     def phi_pack(buffer, section):
         for side, start in ((0, PAD), (1, PAD + cells - 2)):
@@ -388,9 +426,6 @@
             for k in range(variables):
                 out_ref[k, r, into, :] = total[k]
 
-    def each(low, high, step):
-        lax.fori_loop(low, high, lambda r, _: (step(r), 0)[1], 0)
-
     def each_pair(low, high, step):
         def both(i):
             step(2 * i)
@@ -398,16 +433,20 @@
 
         each(low // 2, high // 2, both)
 
-    each_pair(0, rows, early_one)
-    each(0, 2, lambda i: radial_store(first, 2 + 2 * i, 2))
-    radial_store(first, 6, 1)
-
     pl.semaphore_wait(barrier, greeted)
+    pl.when(turned_to)(lambda: signal(turn, radial_peer(1)))
+
+    def reply(v):
+        pl.when(v < slab)(lambda: signal(far.at[jnp.where(z < TOP, 0, 1)], (v, wedge)))
 
     part_copies = [
-        remote(part, got_part.at[j], part_send.at[j], part_recv.at[j], phi_peer(j))
+        remote(part, got_part.at[j], part_send.at[0], part_recv.at[0], phi_peer(j))
         for j in range(1, wedges)
     ]
+    others = pl.ds(1, wedges - 1)
+    part_all = remote(
+        got_part.at[others], got_part.at[others], part_send.at[0], part_recv.at[0], phi_peer(1)
+    )
     first_radial, second_radial = radial_copies(first, 0), radial_copies(second, 1)
     first_phi, second_phi = phi_copies(0), phi_copies(1)
     for copy in part_copies:
@@ -415,57 +454,97 @@
     radial_start(first_radial)
     for copy in first_phi:
         copy.start()
+    each_slab(0, level, reply)
     got_part[0] = part[...]
-    for copy in part_copies:
-        copy.wait_recv()
+    each_pair(0, rows, early_one)
+    each(0, 2, lambda i: radial_store(first, 2 + 2 * i, 2))
+    radial_store(first, 6, 1)
+    part_all.wait_recv()
     shells = jnp.zeros((1, lanes), jnp.float32)
     for w in range(wedges):
         shells = shells + got_part[lax.rem(wedge + wedges - w, wedges)]
     slab_part[...] = shells
 
-    def slab_copy(j):
+    def slab_copy(source, target):
         return remote(
-            slab_part, got.at[j], slab_send.at[j], slab_recv.at[j], radial_peer(j)
+            slab_part, got.at[source], slab_send.at[0], slab_recv.at[0], (target, wedge),
         )
 
+    def slab_all(count):
+        ref = got.at[pl.ds(0, count)]
+        return remote(ref, ref, slab_send.at[0], slab_recv.at[0], radial_peer(0))
+
+    def by_slab(low, high, step):
+        if high - low == 1:
+            step(low)
+            return
+        middle = (low + high) // 2
+        pl.when(slab < middle)(lambda: by_slab(low, middle, step))
+        pl.when(slab >= middle)(lambda: by_slab(middle, high, step))
+
+    def slab_start(v):
+        pl.when(v > slab)(lambda: slab_copy(slab, v).start())
+
     above_copy = remote(
-        slab_part, got_above, above_send.at[0], above_recv.at[0], radial_peer(-1)
+        slab_part, got_above, slab_send.at[0], above_recv.at[0], radial_peer(-1)
     )
-    each(1, slabs - slab, lambda j: slab_copy(j).start())
-    pl.when(has_down)(above_copy.start)
-
-    for copy in first_phi:
-        copy.wait_recv()
+    each_slab(0, level + 1, slab_start)
+    pl.when(plain_down)(above_copy.start)
+
+    @pl.when(turns)
+    def _():
+        pl.semaphore_wait(turn, 1)
+        first_radial[1].start()
+        above_copy.start()
+
+    def send_out():
+        for at in range(2):
+            @pl.when(heard[at] > 0)
+            def _():
+                pl.semaphore_wait(far.at[at], heard[at])
+
+        each_slab(level + 1, levels, slab_start)
+
+    phi_both(0).wait_recv()
     phi_unpack(first, 0)
+    pl.when(turns)(send_out)
     radial_land(first_radial)
     radial_ends(first)
     phi_ends(first)
     each(0, 2, lambda i: radial_store(first, 7 * i, 2))
-    each(0, rows, late_one)
+    each(0, 4, lambda i: late_one(i + (i // 2) * (rows - 4)))
+    radial_sent(first_radial)
+    radial_start(second_radial)
+    pl.when(turns)(second_radial[1].start)
+    each(2, rows - 2, late_one)
     phi_pack(second, 1)
-    radial_start(second_radial)
     for copy in second_phi:
         copy.start()
+
+    pl.when(jnp.logical_not(turns))(send_out)
 
     after = jnp.where(lane < line, 1.0, jnp.where(lane == line, 0.5, 0.0))
     within = jnp.sum(after * slab_part[...], axis=1, keepdims=True)
     whole = jnp.sum(jnp.where(line >= 0, slab_part[...], 0.0), axis=1, keepdims=True)
 
-    for copy in second_phi:
-        copy.wait_recv()
+    phi_both(1).wait_recv()
     phi_unpack(second, 1)
     radial_land(second_radial)
 
+    part_all.wait_send()
+    phi_both(0).wait_send()
+    phi_both(1).wait_send()
     radial_sent(second_radial)
+    by_slab(0, slabs, lambda s: slab_all(slabs - max(s, 1)).wait_send())
     pl.when(has_up)(above_copy.wait_recv)
-    each(1, slab + 1, lambda j: slab_copy(j).wait_recv())
+    by_slab(0, slabs, lambda s: slab_all(s).wait_recv() if s else None)
     sums = [jnp.zeros((1, lanes), jnp.float32) for _ in range(4)]
-    for j in range(1, slabs):
-        sums[j % 4] = sums[j % 4] + jnp.where(slab >= j, got[j], 0.0)
+    for v in range(slabs - 1):
+        sums[v % 4] = sums[v % 4] + jnp.where(slab > v, got[v], 0.0)
     before = jnp.broadcast_to((sums[0] + sums[1]) + (sums[2] + sums[3]), (rows, lanes))
     before = core[0] + jnp.sum(before, axis=1, keepdims=True)
     inner = jnp.where(lane > line, 1.0, jnp.where(lane == line, 0.5, 0.0))
-    inner = jnp.sum(inner * got[1], axis=1, keepdims=True)
+    inner = jnp.sum(inner * got[jnp.maximum(slab - 1, 0)], axis=1, keepdims=True)
     outer = jnp.sum(after * got_above[...], axis=1, keepdims=True)
     wide = jnp.zeros((rows, lanes), jnp.float32)
     enclosed = before + within + wide
@@ -491,12 +570,6 @@
     phi_ends(second)
     radial_store(second, 0, 1)
     each(0, rows, section_two)
-
-    for copy in part_copies + first_phi + second_phi:
-        copy.wait_send()
-    radial_sent(first_radial)
-    each(1, slabs - slab, lambda j: slab_copy(j).wait_send())
-    pl.when(has_down)(above_copy.wait_send)
 
 
 def body(conserved, core_mass):
@@ -530,15 +603,16 @@
             pltpu.VMEM((3 * TILE, lanes), jnp.float32),
             pltpu.VMEM((TILE, lanes), jnp.float32),
             pltpu.SMEM((1,), jnp.float32),
+            pltpu.SemaphoreType.REGULAR((2,)),
+            pltpu.SemaphoreType.REGULAR,
             dma((3,)),
+            dma((2,)),
             dma((4,)),
-            dma((4,)),
-            dma((4,)),
-            dma((4,)),
-            dma((wedges,)),
-            dma((wedges,)),
-            dma((slabs,)),
-            dma((slabs,)),
+            dma((2,)),
+            dma((2,)),
+            dma((1,)),
+            dma((1,)),
+            dma((1,)),
             dma((1,)),
             dma((1,)),
         ],

time: 30 us -> 26.7 us (0.89)
  the two profiles are of different devices: /device:TPU:1 before, /device:TPU:2 now
where the time goes in v2:
time: 26.7 us; the launch traced here: 26.3 us
  Pallas kernels  23.7 us (89%)
  local copies, waits for them, and re-layouts  1.31 us (5%)
  between operations  1.28 us (5%)
    pallas_call x1, Pallas kernels, body(): pl.pallas_call(functools.partial(kernel, sizes, (slabs, wedges)), out_sha...  23.7 us
    unnamed x2, local copies, waits for them, and re-layouts  1.31 us

profile of v2, /device:TPU:2, one launch (start us, length us, event | category | flops | bytes accessed | tf_op | source)
XLA Modules:
  0.0 26.3 jit_solution(6657962404361141393)
XLA Ops:
  1.3 23.7 %shard_map.50 = (f32[8,8,16,128]{3,2,1,0:T(8,128)S(1)}, f32[1,8]{1,0:T(1,128)S(1)}) custom-call(f32[1]{0:T(128)S(6)} %copy.9.core_ref, f32[8,128]{1,0:T(8,128)} %constant.2.clone.table_ref, f32[8,8,16,128]{3,2,1,0:T(8,128)} %input_ref.1), custom_call_target="tpu_custom_call" | custom-call | tf_op jit(solution)/shard_map/pallas_call | solution.py:583
  25.0 0.8 %copy.7 = f32[8,8,16,128]{3,2,1,0:T(8,128)} copy(f32[8,8,16,128]{3,2,1,0:T(8,128)S(1)} %get-tuple-element.6) | data formatting | bytes 1048576
  25.8 0.5 %copy.8 = f32[8]{0:T(128)} copy(f32[8]{0:T(128)S(1)} %bitcast.1) | data formatting | bytes 64

commit v3 on v2

--- a/solution.py
+++ b/solution.py
@@ -102,7 +102,7 @@
     table,
     core,
     far,
-    turn,
+    told,
     load_sem,
     radial_send,
     radial_recv,
@@ -147,8 +147,8 @@
     rank = jnp.where(z < TOP, 2 * x + c, 2 * (z - TOP) + c)
     span, levels = slabs // DEPTH, DEPTH
     turns = jnp.logical_and(slab % LINE == 0, has_down)
-    turned_to = jnp.logical_and(slab % LINE == LINE - 1, has_up)
-    plain_down = jnp.logical_and(has_down, jnp.logical_not(turns))
+    turned_last = slab % LINE == LINE - 1
+    turned_to = jnp.logical_and(turned_last, has_up)
 
     def signal(semaphore, peer):
         pl.semaphore_signal(semaphore, inc=1, device_id=peer, device_id_type=MESH)
@@ -167,13 +167,19 @@
     def greet_level(v):
         pl.when(jnp.logical_or(v < slab, v == slab + 1))(lambda: greet(v))
 
+    def greet_outer(v):
+        known = jnp.logical_or(v % LINE != LINE - 1, v == slab - 1)
+        pl.when(known)(lambda: greet(v))
+
     for j in range(1, wedges):
         signal(barrier, phi_peer(j))
     pl.when(jnp.logical_and(z > 0, jnp.logical_and(z <= TOP, c == 0)))(lambda: greet(slab - 1))
+    pl.when(turned_to)(lambda: greet(slab + 1))
     each_slab(level, level + 1, greet_level)
-    each_slab(level + 1, levels, greet)
+    each_slab(level + 1, levels, greet_outer)
     inside = jnp.where(z < TOP, 2 * c, jnp.where(rank > 0, 1, 0))
-    greeted = (wedges - 1) + span * level + (span - 1 - rank) + inside
+    inside = jnp.where(turned_last, jnp.where(has_up, 2, 1), span * level + span - 1 - rank + inside)
+    greeted = (wedges - 1) + inside + jnp.where(turns, 1, 0)
     further = slabs // LINE - 1 - x
     heard = (
         jnp.where(z < TOP, (TOP - 1 - z) * 2 * (further + 1), 0),
@@ -205,7 +211,7 @@
     def radial_start(copies):
         up, down = copies
         pl.when(has_up)(up.start)
-        pl.when(plain_down)(down.start)
+        pl.when(has_down)(down.start)
 
     def radial_sent(copies):
         up, down = copies
@@ -434,7 +440,6 @@
         each(low // 2, high // 2, both)
 
     pl.semaphore_wait(barrier, greeted)
-    pl.when(turned_to)(lambda: signal(turn, radial_peer(1)))
 
     def reply(v):
         pl.when(v < slab)(lambda: signal(far.at[jnp.where(z < TOP, 0, 1)], (v, wedge)))
@@ -454,11 +459,23 @@
     radial_start(first_radial)
     for copy in first_phi:
         copy.start()
-    each_slab(0, level, reply)
+
+    pl.when(slab % LINE == LINE - 2)(lambda: signal(told, (slab + 1, wedge)))
+
+    @pl.when(jnp.logical_not(turned_last))
+    def _():
+        each_slab(0, level, reply)
+
     got_part[0] = part[...]
     each_pair(0, rows, early_one)
     each(0, 2, lambda i: radial_store(first, 2 + 2 * i, 2))
     radial_store(first, 6, 1)
+
+    @pl.when(turned_last)
+    def _():
+        pl.semaphore_wait(told, 1)
+        each_slab(0, level, reply)
+
     part_all.wait_recv()
     shells = jnp.zeros((1, lanes), jnp.float32)
     for w in range(wedges):
@@ -489,21 +506,14 @@
         slab_part, got_above, slab_send.at[0], above_recv.at[0], radial_peer(-1)
     )
     each_slab(0, level + 1, slab_start)
-    pl.when(plain_down)(above_copy.start)
-
-    @pl.when(turns)
-    def _():
-        pl.semaphore_wait(turn, 1)
-        first_radial[1].start()
-        above_copy.start()
+    pl.when(has_down)(above_copy.start)
 
     def send_out():
-        for at in range(2):
+        for at, low, high in ((0, level + 1, TOP), (1, jnp.maximum(level + 1, TOP), levels)):
             @pl.when(heard[at] > 0)
             def _():
                 pl.semaphore_wait(far.at[at], heard[at])
-
-        each_slab(level + 1, levels, slab_start)
+                each_slab(low, high, slab_start)
 
     phi_both(0).wait_recv()
     phi_unpack(first, 0)
@@ -515,7 +525,6 @@
     each(0, 4, lambda i: late_one(i + (i // 2) * (rows - 4)))
     radial_sent(first_radial)
     radial_start(second_radial)
-    pl.when(turns)(second_radial[1].start)
     each(2, rows - 2, late_one)
     phi_pack(second, 1)
     for copy in second_phi:
@@ -569,7 +578,7 @@
 
     phi_ends(second)
     radial_store(second, 0, 1)
-    each(0, rows, section_two)
+    each_pair(0, rows, section_two)
 
 
 def body(conserved, core_mass):

time: 26.7 us -> 24.5 us (0.918)
  Pallas kernels: 23.7 us -> 21.8 us
    pallas_call x1, Pallas kernels: 23.7 us -> 21.8 us  [body(): pl.pallas_call(functools.partial(kernel, sizes, (slabs, wedges)), out_sha...]
where the time goes in v3:
time: 24.5 us; the launch traced here: 24.4 us
  Pallas kernels  21.8 us (89%)
  local copies, waits for them, and re-layouts  1.31 us (5%)
  between operations  1.28 us (5%)
    pallas_call x1, Pallas kernels, body(): pl.pallas_call(functools.partial(kernel, sizes, (slabs, wedges)), out_sha...  21.8 us
    unnamed x2, local copies, waits for them, and re-layouts  1.31 us

profile of v3, /device:TPU:2, one launch (start us, length us, event | category | flops | bytes accessed | tf_op | source)
XLA Modules:
  0.0 24.4 jit_solution(6769223012203611309)
XLA Ops:
  1.3 21.8 %shard_map.50 = (f32[8,8,16,128]{3,2,1,0:T(8,128)S(1)}, f32[1,8]{1,0:T(1,128)S(1)}) custom-call(f32[1]{0:T(128)S(6)} %copy.9.core_ref, f32[8,128]{1,0:T(8,128)} %constant.2.clone.table_ref, f32[8,8,16,128]{3,2,1,0:T(8,128)} %input_ref.1), custom_call_target="tpu_custom_call" | custom-call | tf_op jit(solution)/shard_map/pallas_call | solution.py:592
  23.1 0.8 %copy.7 = f32[8,8,16,128]{3,2,1,0:T(8,128)} copy(f32[8,8,16,128]{3,2,1,0:T(8,128)S(1)} %get-tuple-element.6) | data formatting | bytes 1048576
  23.9 0.5 %copy.8 = f32[8]{0:T(128)} copy(f32[8]{0:T(128)S(1)} %bitcast.1) | data formatting | bytes 64

commit v4 on v3

v4 whole, which is shorter than its diff:
```python
import functools
import math
import types

import jax
import jax.numpy as jnp
import numpy as np
from jax import lax
from jax.experimental import pallas as pl
from jax.experimental.pallas import tpu as pltpu
from jax.sharding import PartitionSpec as P

ADIABATIC = 4.0 / 3.0
INNER_RADIUS = 1.0
OUTER_RADIUS = 2.0
COURANT = 0.4
GRAVITY_KICK = 0.004
MINIMUM_DENSITY = 0.05
PRESSURE_FLOOR = 0.01
MESH = pl.DeviceIdType.MESH
TILE = 8
PAD = 8
DEPTH = 8
LINE = 2 * DEPTH
TOP = 4


def step_sizes(radial_total, phi_total, theta_total):
    theta_step = math.pi / theta_total
    phi_step = 2.0 * math.pi / phi_total
    polar_width = INNER_RADIUS * math.sin(0.5 * theta_step) * phi_step
    radial_step = min(2.0 * polar_width, (OUTER_RADIUS - INNER_RADIUS) / radial_total)
    timestep = COURANT * min(radial_step, polar_width)
    return (radial_step, theta_step, phi_step, timestep)


def angle_tables(theta_cells, theta_step):
    step = np.float32(theta_step)
    centre = (np.arange(theta_cells, dtype=np.float32) + np.float32(0.5)) * step
    face = np.arange(theta_cells + 1, dtype=np.float32) * step
    sine = np.sin(centre.astype(np.float64))
    cosine = np.cos(centre.astype(np.float64))
    face_sine = np.sin(face.astype(np.float64))
    face_sine[-1] = 0.0
    zero = np.zeros(theta_cells)
    upper = 0.5 * face_sine[1:] / theta_step
    rows = [sine, upper, cosine / sine, 1.0 / sine, zero, zero, zero, zero]
    return np.stack(rows).astype(np.float32)


def half_slope(below, above):
    high, low = jnp.maximum(below, 0.0), jnp.minimum(below, 0.0)
    return 0.5 * jnp.maximum(jnp.minimum(above, high), low)


def thermo(q):
    density = jnp.maximum(q[0], MINIMUM_DENSITY)
    inverse = 1.0 / density
    kinetic = 0.5 * (q[1] * q[1] + q[2] * q[2] + q[3] * q[3]) * inverse
    pressure = jnp.maximum((ADIABATIC - 1.0) * (q[4] - kinetic), PRESSURE_FLOOR * density)
    return density, inverse, pressure


def physical(q, component):
    _, inverse, pressure = thermo(q)
    normal = q[component] * inverse
    squared = ADIABATIC * pressure * inverse
    return normal, pressure, jnp.abs(normal) + squared * lax.rsqrt(squared)


def flux(left, right, component, half_area):
    left_v, left_p, left_a = physical(left, component)
    right_v, right_p, right_a = physical(right, component)
    signal = jnp.maximum(left_a, right_a)
    left_w = half_area * (left_v + signal)
    right_w = half_area * (right_v - signal)
    out = [a * left_w + b * right_w for a, b in zip(left, right)]
    out[component] = out[component] + half_area * (left_p + right_p)
    out[4] = out[4] + half_area * (left_p * left_v + right_p * right_v)
    return out


def each(low, high, step):
    lax.fori_loop(low, high, lambda r, _: (step(r), 0)[1], 0)


def each_pair(low, high, step):
    def both(i):
        step(2 * i)
        step(2 * i + 1)

    each(low // 2, high // 2, both)


def stencils(sizes, extent, slab, table, ends, radial):
    radial_step, theta_step, phi_step, _ = sizes
    variables, rows, cells, lanes = extent
    tiles = cells // TILE
    shape = (TILE, lanes)
    sub = lax.broadcasted_iota(jnp.int32, shape, 0)
    lane_tile = lax.broadcasted_iota(jnp.int32, shape, 1)
    is_last = lane_tile == lanes - 1
    is_top, is_bottom = sub == TILE - 1, sub == 0

    def spread(value):
        return jnp.broadcast_to(value, shape)

    def radius_of(index):
        index = jnp.full(shape, slab * rows + index, jnp.int32).astype(jnp.float32)
        return INNER_RADIUS + (index + 0.5) * radial_step

    def radial_faces(buffer, low, count, tile):
        where = pl.ds(PAD + TILE * tile, TILE)
        lefts = [[] for _ in range(count)]
        rights = [[] for _ in range(count)]
        for k in range(variables):
            q = [buffer[k, low + j, where, :] for j in range(count + 3)]
            step = [q[j + 1] - q[j] for j in range(count + 2)]
            slope = [half_slope(step[j], step[j + 1]) for j in range(count + 1)]
            for i in range(count):
                lefts[i].append(q[i + 1] + slope[i])
                rights[i].append(q[i + 2] - slope[i + 1])
        out = []
        for i in range(count):
            face = radius_of(low + i) - 0.5 * radial_step
            out.append(flux(lefts[i], rights[i], 1, face * face * (0.5 / radial_step)))
        return out

    def radial_store(buffer, low, count):
        for t in range(tiles):
            for i, face in enumerate(radial_faces(buffer, low, count, t)):
                for k in range(variables):
                    radial[k, low + i, pl.ds(TILE * t, TILE), :] = face[k]

    def theta_part(centre):
        left, right = [], []
        for q in centre:
            after = pltpu.roll(q, lanes - 1, 1)
            above = jnp.where(is_last, 0.0, after - q)
            below = pltpu.roll(above, 1, 1)
            slope = half_slope(below, above)
            left.append(q + slope)
            right.append(pltpu.roll(q - slope, lanes - 1, 1))
        upper = flux(left, right, 2, spread(table[1:2, :]))
        return [pltpu.roll(f, 1, 1) - f for f in upper]

    def phi_ends(buffer):
        def column_at(k, cell):
            return buffer[k, pl.ds(2, rows), PAD + cell, :]

        left, right = [], []
        for k in range(variables):
            a, b, c, d = (column_at(k, cell) for cell in (-2, -1, 0, 1))
            left.append(b + half_slope(b - a, c - b))
            right.append(c - half_slope(c - b, d - c))
            a, b, c = (column_at(k, cell) for cell in (cells - 1, cells, cells + 1))
            ends[1, k] = b - half_slope(b - a, c - b)
        for k, f in enumerate(flux(left, right, 3, 0.5 / phi_step)):
            ends[0, k] = f

    def phi_part(buffer, r):
        left, right = [[] for _ in range(tiles)], [[] for _ in range(tiles)]
        for k in range(variables):
            turned = []
            for t in range(tiles):
                start = PAD + TILE * t
                a, b, c = (
                    buffer[k, r + 2, pl.ds(start + offset, TILE), :] for offset in (-1, 0, 1)
                )
                slope = half_slope(b - a, c - b)
                left[t].append(b + slope)
                turned.append(pltpu.roll(b - slope, TILE - 1, 0))
            turned.append(spread(ends[1, k, pl.ds(r, 1), :]))
            for t in range(tiles):
                right[t].append(jnp.where(is_top, turned[t + 1], turned[t]))
        upper = [flux(left[t], right[t], 3, 0.5 / phi_step) for t in range(tiles)]
        out = [[] for _ in range(tiles)]
        for k in range(variables):
            before = spread(ends[0, k, pl.ds(r, 1), :])
            for t in range(tiles):
                turned = pltpu.roll(upper[t][k], 1, 0)
                out[t].append(jnp.where(is_bottom, before, turned) - upper[t][k])
                before = turned
        return out

    def sources(centre, inverse_r):
        density, inverse, pressure = thermo(centre)
        vr, vt, vp = (centre[m] * inverse for m in (1, 2, 3))
        cot = spread(table[2:3, :])
        swirl = density * vp * vp
        return density, [
            (2.0 * pressure + density * vt * vt + swirl) * inverse_r,
            ((pressure + swirl) * cot - density * vr * vt) * inverse_r,
            -density * vp * (vr + vt * cot) * inverse_r,
        ]

    def centre_at(buffer, r, tile):
        return [
            buffer[k, r + 2, pl.ds(PAD + TILE * tile, TILE), :] for k in range(variables)
        ]

    return types.SimpleNamespace(
        spread=spread,
        radius_of=radius_of,
        radial_faces=radial_faces,
        radial_store=radial_store,
        theta_part=theta_part,
        phi_ends=phi_ends,
        phi_part=phi_part,
        sources=sources,
        centre_at=centre_at,
    )


def kernel(
    sizes,
    counts,
    core_ref,
    table_ref,
    input_ref,
    first,
    second,
    pull,
    table,
    mass_ref,
    edge,
    halo,
    radial,
    ends,
    part,
    slab_part,
    got_part,
    got,
    got_above,
    core,
    far,
    told,
    load_sem,
    radial_send,
    radial_recv,
    phi_send,
    phi_recv,
    part_send,
    part_recv,
    slab_send,
    slab_recv,
    above_recv,
):
    radial_step, theta_step, phi_step, timestep = sizes
    slabs, wedges = counts
    variables, rows, cells, lanes = input_ref.shape
    tiles = cells // TILE
    strength = GRAVITY_KICK / timestep
    slab, wedge = lax.axis_index("radial"), lax.axis_index("phi")
    has_up, has_down = slab < slabs - 1, slab > 0
    shape = (TILE, lanes)

    load = pltpu.make_async_copy(
        input_ref, first.at[:, pl.ds(2, rows), pl.ds(PAD, cells), :], load_sem.at[0]
    )
    load.start()
    load_table = pltpu.make_async_copy(table_ref, table, load_sem.at[1])
    load_table.start()
    load_core = pltpu.make_async_copy(core_ref, core, load_sem.at[2])
    load_core.start()

    def radial_peer(jump):
        return (slab + jump, wedge)

    def phi_peer(jump):
        return (slab, lax.rem(wedge + jump, wedges))

    barrier = pltpu.get_barrier_semaphore()
    x, z, c = slab // LINE, (slab // 2) % DEPTH, slab % 2
    level = jnp.where(z < TOP, z, TOP + x)
    rank = jnp.where(z < TOP, 2 * x + c, 2 * (z - TOP) + c)
    span, levels = slabs // DEPTH, DEPTH
    turns = jnp.logical_and(slab % LINE == 0, has_down)
    turned_last = slab % LINE == LINE - 1
    turned_to = jnp.logical_and(turned_last, has_up)

    def signal(semaphore, peer):
        pl.semaphore_signal(semaphore, inc=1, device_id=peer, device_id_type=MESH)

    def each_slab(low, high, step):
        def one_level(at):
            for i in range(span):
                spread_out = LINE * (i // 2) + 2 * at + i % 2
                step(jnp.where(at < TOP, spread_out, LINE * (at - TOP) + LINE // 2 + i))

        each(low, high, one_level)

    def greet(v):
        signal(barrier, (v, wedge))

    def greet_level(v):
        pl.when(jnp.logical_or(v < slab, v == slab + 1))(lambda: greet(v))

    def greet_outer(v):
        known = jnp.logical_or(v % LINE != LINE - 1, v == slab - 1)
        pl.when(known)(lambda: greet(v))

    for j in range(1, wedges):
        signal(barrier, phi_peer(j))
    pl.when(jnp.logical_and(z > 0, jnp.logical_and(z <= TOP, c == 0)))(lambda: greet(slab - 1))
    pl.when(turned_to)(lambda: greet(slab + 1))
    each_slab(level, level + 1, greet_level)
    each_slab(level + 1, levels, greet_outer)
    inside = jnp.where(z < TOP, 2 * c, jnp.where(rank > 0, 1, 0))
    inside = jnp.where(turned_last, jnp.where(has_up, 2, 1), span * level + span - 1 - rank + inside)
    greeted = (wedges - 1) + inside + jnp.where(turns, 1, 0)
    further = slabs // LINE - 1 - x
    heard = (
        jnp.where(z < TOP, (TOP - 1 - z) * 2 * (further + 1), 0),
        jnp.where(z < TOP, (DEPTH - TOP) * 2 * (further + 1), span * further),
    )

    load.wait()
    load_table.wait()
    load_core.wait()

    def remote(src, dst, send, recv, peer):
        return pltpu.make_async_remote_copy(
            src_ref=src, dst_ref=dst, send_sem=send, recv_sem=recv, device_id=peer,
            device_id_type=MESH,
        )

    def radial_copies(buffer, section):
        where, slot = pl.ds(PAD, cells), 2 * section
        up = remote(
            buffer.at[:, pl.ds(rows, 2), where, :], buffer.at[:, pl.ds(0, 2), where, :],
            radial_send.at[0], radial_recv.at[slot], radial_peer(1),
        )
        down = remote(
            buffer.at[:, pl.ds(2, 2), where, :], buffer.at[:, pl.ds(rows + 2, 2), where, :],
            radial_send.at[1], radial_recv.at[slot + 1], radial_peer(-1),
        )
        return up, down

    def radial_start(copies):
        up, down = copies
        pl.when(has_up)(up.start)
        pl.when(has_down)(down.start)

    def radial_sent(copies):
        up, down = copies
        pl.when(has_up)(up.wait_send)
        pl.when(has_down)(down.wait_send)

    def radial_land(copies):
        up, down = copies
        pl.when(has_down)(up.wait_recv)
        pl.when(has_up)(down.wait_recv)

    def radial_ends(buffer):
        for t in range(tiles):
            where = pl.ds(PAD + TILE * t, TILE)

            @pl.when(jnp.logical_not(has_down))
            def _():
                value = buffer[:, 2, where, :]
                buffer[:, 0, where, :] = value
                buffer[:, 1, where, :] = value

            @pl.when(jnp.logical_not(has_up))
            def _():
                value = buffer[:, rows + 1, where, :]
                buffer[:, rows + 2, where, :] = value
                buffer[:, rows + 3, where, :] = value

    whole, inside_rows, edge_rows = [(0, rows)], [(2, rows - 4)], [(0, 2), (rows - 2, 2)]

    def phi_copies(section, count):
        slot = 2 * section
        return [
            remote(
                edge.at[slot + side, :, pl.ds(0, count)],
                halo.at[slot + side, :, pl.ds(0, count)],
                phi_send.at[section], phi_recv.at[section], phi_peer(jump),
            )
            for side, jump in ((0, wedges - 1), (1, 1))
        ]

    def phi_both(section, count):
        where = (pl.ds(2 * section, 2), slice(None), pl.ds(0, count))
        return remote(
            edge.at[where], halo.at[where], phi_send.at[section], phi_recv.at[section],
            phi_peer(1),
        )

    def phi_pack(buffer, section, pieces):
        for side, start in ((0, PAD), (1, PAD + cells - 2)):
            at = 0
            for begin, count in pieces:
                edge[section * 2 + side, :, pl.ds(at, count)] = buffer[
                    :, pl.ds(2 + begin, count), pl.ds(start, 2), :
                ]
                at += count

    def phi_unpack(buffer, section, pieces):
        for side, start in ((0, PAD + cells), (1, PAD - 2)):
            at = 0
            for begin, count in pieces:
                buffer[:, pl.ds(2 + begin, count), pl.ds(start, 2), :] = halo[
                    section * 2 + side, :, pl.ds(at, count)
                ]
                at += count

    lane = lax.broadcasted_iota(jnp.int32, (rows, lanes), 1)
    line = lax.broadcasted_iota(jnp.int32, (rows, lanes), 0)
    column = jnp.sum(first[0, pl.ds(2, rows), pl.ds(PAD, cells), :], axis=1)
    column = jnp.sum(column * table[0:1, :], axis=1, keepdims=True)
    centres = INNER_RADIUS + (
        (slab * rows + line).astype(jnp.float32) + 0.5
    ) * radial_step
    column = column * centres * centres * (radial_step * theta_step * phi_step)
    part[...] = jnp.sum(jnp.where(lane == line, column, 0.0), axis=0, keepdims=True)
    phi_pack(first, 0, whole)

    on = stencils(sizes, input_ref.shape, slab, table, ends, radial)

    def early_one(r):
        inverse_r = 1.0 / on.radius_of(r)
        around = inverse_r * on.spread(table[3:4, :]) * timestep
        for t in range(tiles):
            centre = on.centre_at(first, r, t)
            total = [c + d * around for c, d in zip(centre, on.theta_part(centre))]
            _, source = on.sources(centre, inverse_r)
            for m in range(3):
                total[m + 1] = total[m + 1] + timestep * source[m]
            for k in range(variables):
                second[k, r + 2, pl.ds(PAD + TILE * t, TILE), :] = total[k]

    def late_one(r):
        inverse_r = 1.0 / on.radius_of(r)
        around = inverse_r * on.spread(table[3:4, :]) * timestep
        along = inverse_r * inverse_r * timestep
        for t, part_of in enumerate(on.phi_part(first, r)):
            into = pl.ds(TILE * t, TILE)
            where = pl.ds(PAD + TILE * t, TILE)
            for k in range(variables):
                across = radial[k, r, into, :] - radial[k, r + 1, into, :]
                second[k, r + 2, where, :] = (
                    second[k, r + 2, where, :] + part_of[k] * around + across * along
                )

    pl.semaphore_wait(barrier, greeted)

    def reply(v):
        pl.when(v < slab)(lambda: signal(far.at[jnp.where(z < TOP, 0, 1)], (v, wedge)))

    part_copies = [
        remote(part, got_part.at[j], part_send.at[0], part_recv.at[0], phi_peer(j))
        for j in range(1, wedges)
    ]
    others = pl.ds(1, wedges - 1)
    part_all = remote(
        got_part.at[others], got_part.at[others], part_send.at[0], part_recv.at[0], phi_peer(1)
    )
    first_radial, second_radial = radial_copies(first, 0), radial_copies(second, 1)
    first_phi = phi_copies(0, rows)
    inside_phi, edge_phi = phi_copies(1, rows - 4), phi_copies(2, 4)
    for copy in part_copies:
        copy.start()
    radial_start(first_radial)
    for copy in first_phi:
        copy.start()

    pl.when(slab % LINE == LINE - 2)(lambda: signal(told, (slab + 1, wedge)))

    @pl.when(jnp.logical_not(turned_last))
    def _():
        each_slab(0, level, reply)

    got_part[0] = part[...]
    each_pair(0, rows, early_one)
    each(0, 2, lambda i: on.radial_store(first, 2 + 2 * i, 2))
    on.radial_store(first, 6, 1)

    @pl.when(turned_last)
    def _():
        pl.semaphore_wait(told, 1)
        each_slab(0, level, reply)

    part_all.wait_recv()
    shells = jnp.zeros((1, lanes), jnp.float32)
    for w in range(wedges):
        shells = shells + got_part[lax.rem(wedge + wedges - w, wedges)]
    slab_part[...] = shells

    def slab_copy(source, target):
        return remote(
            slab_part, got.at[source], slab_send.at[0], slab_recv.at[0], (target, wedge),
        )

    def slab_all(count):
        ref = got.at[pl.ds(0, count)]
        return remote(ref, ref, slab_send.at[0], slab_recv.at[0], radial_peer(0))

    def by_slab(low, high, step):
        if high - low == 1:
            step(low)
            return
        middle = (low + high) // 2
        pl.when(slab < middle)(lambda: by_slab(low, middle, step))
        pl.when(slab >= middle)(lambda: by_slab(middle, high, step))

    def slab_start(v):
        pl.when(v > slab)(lambda: slab_copy(slab, v).start())

    above_copy = remote(
        slab_part, got_above, slab_send.at[0], above_recv.at[0], radial_peer(-1)
    )
    each_slab(0, level + 1, slab_start)
    pl.when(has_down)(above_copy.start)

    def send_out():
        for at, low, high in ((0, level + 1, TOP), (1, jnp.maximum(level + 1, TOP), levels)):
            @pl.when(heard[at] > 0)
            def _():
                pl.semaphore_wait(far.at[at], heard[at])
                each_slab(low, high, slab_start)

    phi_both(0, rows).wait_recv()
    phi_unpack(first, 0, whole)
    on.phi_ends(first)
    each(2, rows - 2, late_one)
    phi_pack(second, 1, inside_rows)
    for copy in inside_phi:
        copy.start()
    pl.when(turns)(send_out)
    radial_land(first_radial)
    radial_ends(first)
    each(0, 2, lambda i: on.radial_store(first, 7 * i, 2))
    each(0, 4, lambda i: late_one(i + (i // 2) * (rows - 4)))
    radial_sent(first_radial)
    radial_start(second_radial)
    phi_pack(second, 2, edge_rows)
    for copy in edge_phi:
        copy.start()
    pl.when(jnp.logical_not(turns))(send_out)

    after = jnp.where(lane < line, 1.0, jnp.where(lane == line, 0.5, 0.0))
    within = jnp.sum(after * slab_part[...], axis=1, keepdims=True)
    whole = jnp.sum(jnp.where(line >= 0, slab_part[...], 0.0), axis=1, keepdims=True)

    phi_both(1, rows - 4).wait_recv()
    phi_unpack(second, 1, inside_rows)
    phi_both(2, 4).wait_recv()
    phi_unpack(second, 2, edge_rows)
    radial_land(second_radial)

    part_all.wait_send()
    phi_both(0, rows).wait_send()
    phi_both(1, rows - 4).wait_send()
    phi_both(2, 4).wait_send()
    radial_sent(second_radial)
    by_slab(0, slabs, lambda s: slab_all(slabs - max(s, 1)).wait_send())
    pl.when(has_up)(above_copy.wait_recv)
    by_slab(0, slabs, lambda s: slab_all(s).wait_recv() if s else None)
    sums = [jnp.zeros((1, lanes), jnp.float32) for _ in range(4)]
    for v in range(slabs - 1):
        sums[v % 4] = sums[v % 4] + jnp.where(slab > v, got[v], 0.0)
    before = jnp.broadcast_to((sums[0] + sums[1]) + (sums[2] + sums[3]), (rows, lanes))
    before = core[0] + jnp.sum(before, axis=1, keepdims=True)
    inner = jnp.where(lane > line, 1.0, jnp.where(lane == line, 0.5, 0.0))
    inner = jnp.sum(inner * got[jnp.maximum(slab - 1, 0)], axis=1, keepdims=True)
    outer = jnp.sum(after * got_above[...], axis=1, keepdims=True)
    wide = jnp.zeros((rows, lanes), jnp.float32)
    enclosed = before + within + wide
    mass_ref[...] = jnp.sum(jnp.where(lane == line, enclosed, 0.0), axis=0, keepdims=True)[:, :rows]
    for i, inside in ((0, before - inner), (1, before + within), (2, before + whole + outer)):
        at = centres + (i - 1) * rows * radial_step
        pull[pl.ds(8 * i, 8), :] = strength * (inside + wide) / (at * at)

    def pulled(row, start):
        where = pl.ds(start, TILE)
        gravity = timestep * on.spread(pull[pl.ds(row + 6, 1), :])
        density = jnp.maximum(first[0, row, where, :], MINIMUM_DENSITY)
        second[1, row, where, :] = second[1, row, where, :] - density * gravity
        second[4, row, where, :] = second[4, row, where, :] - first[1, row, where, :] * gravity

    def pulled_row(row):
        for t in range(-1, tiles + 1):
            pulled(row, PAD + TILE * t)

    each_pair(0, rows + 4, pulled_row)
    radial_ends(second)


def finish(
    sizes,
    first,
    second,
    pull,
    table,
    mass,
    out_ref,
    mass_ref,
    out,
    ends,
    radial,
    sem,
):
    timestep = sizes[3]
    variables, rows, cells, lanes = out.shape
    tiles = cells // TILE
    slab = lax.axis_index("radial")
    on = stencils(sizes, out.shape, slab, table, ends, radial)
    save_mass = pltpu.make_async_copy(mass, mass_ref, sem.at[1])
    save_mass.start()

    def section_two(r):
        inverse_r = 1.0 / on.radius_of(r)
        scale = 0.5 * timestep
        around = inverse_r * on.spread(table[3:4, :]) * scale
        along = inverse_r * inverse_r * scale
        gravity = on.spread(pull[pl.ds(r + 8, 1), :])
        phi = on.phi_part(second, r)
        for t in range(tiles):
            into = pl.ds(TILE * t, TILE)
            where = pl.ds(PAD + TILE * t, TILE)
            centre = on.centre_at(second, r, t)
            theta = on.theta_part(centre)
            density, source = on.sources(centre, inverse_r)
            source[0] = source[0] - density * gravity
            source.append(-centre[1] * gravity)
            total = [
                0.5 * (first[k, r + 2, where, :] + centre[k])
                + (theta[k] + phi[t][k]) * around
                + (radial[k, r, into, :] - radial[k, r + 1, into, :]) * along
                for k in range(variables)
            ]
            for m in range(4):
                total[m + 1] = total[m + 1] + scale * source[m]
            for k in range(variables):
                out[k, r, into, :] = total[k]

    def save(i):
        where = (slice(None), pl.ds(2 * i, 2))
        return pltpu.make_async_copy(out.at[where], out_ref.at[where], sem.at[0])

    def two(i):
        section_two(2 * i)
        section_two(2 * i + 1)
        save(i).start()

    on.phi_ends(second)
    each(0, (rows + 1) // 3, lambda i: on.radial_store(second, 3 * i, 3))
    each(0, rows // 2, two)
    pltpu.make_async_copy(out, out_ref, sem.at[0]).wait()
    save_mass.wait()


def body(conserved, core_mass):
    variables, rows, cells, lanes = conserved.shape
    slabs, wedges = lax.axis_size("radial"), lax.axis_size("phi")
    sizes = step_sizes(rows * slabs, cells * wedges, lanes)
    table = jnp.asarray(angle_tables(lanes, sizes[1]))
    padded = (variables, rows + 4, cells + 2 * PAD, lanes)
    vmem = pl.BlockSpec(memory_space=pltpu.VMEM)
    dma = pltpu.SemaphoreType.DMA
    first, second, pull, table, mass = pl.pallas_call(
        functools.partial(kernel, sizes, (slabs, wedges)),
        out_shape=(
            pltpu.VMEM(padded, jnp.float32),
            pltpu.VMEM(padded, jnp.float32),
            pltpu.VMEM((3 * TILE, lanes), jnp.float32),
            pltpu.VMEM((TILE, lanes), jnp.float32),
            pltpu.VMEM((1, rows), jnp.float32),
        ),
        in_specs=[pl.BlockSpec(memory_space=pl.ANY)] * 3,
        out_specs=(vmem,) * 5,
        scratch_shapes=[
            pltpu.VMEM((6, variables, rows, 2, lanes), jnp.float32),
            pltpu.VMEM((6, variables, rows, 2, lanes), jnp.float32),
            pltpu.VMEM((variables, rows + 1, cells, lanes), jnp.float32),
            pltpu.VMEM((2, variables, rows, lanes), jnp.float32),
            pltpu.VMEM((1, lanes), jnp.float32),
            pltpu.VMEM((1, lanes), jnp.float32),
            pltpu.VMEM((wedges, 1, lanes), jnp.float32),
            pltpu.VMEM((slabs, 1, lanes), jnp.float32),
            pltpu.VMEM((1, lanes), jnp.float32),
            pltpu.SMEM((1,), jnp.float32),
            pltpu.SemaphoreType.REGULAR((2,)),
            pltpu.SemaphoreType.REGULAR,
            dma((3,)),
            dma((2,)),
            dma((4,)),
            dma((3,)),
            dma((3,)),
            dma((1,)),
            dma((1,)),
            dma((1,)),
            dma((1,)),
            dma((1,)),
        ],
        compiler_params=pltpu.CompilerParams(collective_id=0, has_side_effects=True),
    )(core_mass, table, conserved)
    advanced, mass = pl.pallas_call(
        functools.partial(finish, sizes),
        out_shape=(
            jax.ShapeDtypeStruct(conserved.shape, jnp.float32),
            jax.ShapeDtypeStruct((1, rows), jnp.float32),
        ),
        in_specs=[vmem] * 5,
        out_specs=(pl.BlockSpec(memory_space=pltpu.HBM),) * 2,
        scratch_shapes=[
            pltpu.VMEM(conserved.shape, jnp.float32),
            pltpu.VMEM((2, variables, rows, lanes), jnp.float32),
            pltpu.VMEM((variables, rows + 1, cells, lanes), jnp.float32),
            dma((2,)),
        ],
        compiler_params=pltpu.CompilerParams(vmem_limit_bytes=16 * 1024 * 1024),
    )(first, second, pull, table, mass)
    return advanced, mass.reshape(rows)


def solution(mesh):
    in_specs = (P(None, "radial", "phi", None), P())
    out_specs = (P(None, "radial", "phi", None), P("radial"))
    return jax.shard_map(body, mesh=mesh, in_specs=in_specs, out_specs=out_specs, check_vma=False)
```

time: 24.5 us -> 22.8 us (0.931)
  local copies, waits for them, and re-layouts: 1.31 us -> 0 us
  Pallas kernels: 21.8 us -> 21.4 us
    pallas_call x1, Pallas kernels: 21.8 us -> 18.2 us  [body(): pl.pallas_call(functools.partial(kernel, sizes, (slabs, wedges)), out_sha...]
    pallas_call x0 -> x1, Pallas kernels: none -> 3.21 us  [body(): pl.pallas_call(functools.partial(finish, sizes), out_shape=(jax.ShapeDtyp...]
    unnamed x2 -> x0, local copies, waits for them, and re-layouts: 1.31 us -> none
where the time goes in v4:
time: 22.8 us; the launch traced here: 22.7 us
  Pallas kernels  21.4 us (94%)
  between operations  1.28 us (6%)
    pallas_call x1, Pallas kernels, body(): pl.pallas_call(functools.partial(kernel, sizes, (slabs, wedges)), out_sha...  18.2 us
    pallas_call x1, Pallas kernels, body(): pl.pallas_call(functools.partial(finish, sizes), out_shape=(jax.ShapeDtyp...  3.21 us

profile of v4, /device:TPU:2, one launch (start us, length us, event | category | flops | bytes accessed | tf_op | source)
XLA Modules:
  0.0 22.7 jit_solution(5812129935820152711)
XLA Ops:
  1.3 18.2 %shard_map.50 = (f32[8,12,32,128]{3,2,1,0:T(8,128)S(1)}, f32[8,12,32,128]{3,2,1,0:T(8,128)S(1)}, f32[24,128]{1,0:T(8,128)S(1)}, f32[8,128]{1,0:T(8,128)S(1)}, f32[1,8]{1,0:T(1,128)S(1)}) custom-call(f32[1]{0:T(128)S(6)} %copy.5.core_ref, f32[8,128]{1,0:T(8,128)} %constant.2.clone.table_ref, f32[8,8,16,128]{3,2,1,0:T(8,128)} %input_ref.1), custom_call_target="tpu_custom_call" | custom-call | tf_op jit(solution)/shard_map/pallas_call | solution.py:663
  19.5 3.2 %shard_map.51 = (f32[8,8,16,128]{3,2,1,0:T(8,128)}, f32[1,8]{1,0:T(1,128)}) custom-call(f32[8,12,32,128]{3,2,1,0:T(8,128)S(1)} %get-tuple-element.9.first, f32[8,12,32,128]{3,2,1,0:T(8,128)S(1)} %get-tuple-element.10.second, f32[24,128]{1,0:T(8,128)S(1)} %get-tuple-element.11.pull, f32[8,128]{1,0:T(8,128)S(1)} %get-tuple-element.12.table, ...), custom_call_target="tpu_custom_call" | custom-call | tf_op jit(solution)/shard_map/pallas_call | solution.py:700

commit v5 on v4

--- a/solution.py
+++ b/solution.py
@@ -144,16 +144,18 @@
         upper = flux(left, right, 2, spread(table[1:2, :]))
         return [pltpu.roll(f, 1, 1) - f for f in upper]
 
-    def phi_ends(buffer):
-        def column_at(k, cell):
-            return buffer[k, pl.ds(2, rows), PAD + cell, :]
+    def phi_ends(own, other, pulled):
+        def column_at(k, buffer, side, cell):
+            return pulled(k, side, cell, buffer is other, buffer[side, k, cell])
 
         left, right = [], []
         for k in range(variables):
-            a, b, c, d = (column_at(k, cell) for cell in (-2, -1, 0, 1))
+            a, b = (column_at(k, other, 1, cell) for cell in range(2))
+            c, d = (column_at(k, own, 0, cell) for cell in range(2))
             left.append(b + half_slope(b - a, c - b))
             right.append(c - half_slope(c - b, d - c))
-            a, b, c = (column_at(k, cell) for cell in (cells - 1, cells, cells + 1))
+            a = column_at(k, own, 1, 1)
+            b, c = (column_at(k, other, 0, cell) for cell in range(2))
             ends[1, k] = b - half_slope(b - a, c - b)
         for k, f in enumerate(flux(left, right, 3, 0.5 / phi_step)):
             ends[0, k] = f
@@ -223,10 +225,16 @@
     pull,
     table,
     mass_ref,
-    edge,
-    halo,
+    ends,
+    edge_one,
+    halo_one,
+    edge_two,
+    halo_two,
+    edge_inside,
+    halo_inside,
+    edge_end,
+    halo_end,
     radial,
-    ends,
     part,
     slab_part,
     got_part,
@@ -352,59 +360,49 @@
         pl.when(has_down)(up.wait_recv)
         pl.when(has_up)(down.wait_recv)
 
-    def radial_ends(buffer):
+    def bottom_end(buffer):
         for t in range(tiles):
             where = pl.ds(PAD + TILE * t, TILE)
-
-            @pl.when(jnp.logical_not(has_down))
-            def _():
-                value = buffer[:, 2, where, :]
-                buffer[:, 0, where, :] = value
-                buffer[:, 1, where, :] = value
-
-            @pl.when(jnp.logical_not(has_up))
-            def _():
-                value = buffer[:, rows + 1, where, :]
-                buffer[:, rows + 2, where, :] = value
-                buffer[:, rows + 3, where, :] = value
-
-    whole, inside_rows, edge_rows = [(0, rows)], [(2, rows - 4)], [(0, 2), (rows - 2, 2)]
-
-    def phi_copies(section, count):
-        slot = 2 * section
+            value = buffer[:, 2, where, :]
+            buffer[:, 0, where, :] = value
+            buffer[:, 1, where, :] = value
+
+    def top_end(buffer):
+        for t in range(tiles):
+            where = pl.ds(PAD + TILE * t, TILE)
+            value = buffer[:, rows + 1, where, :]
+            buffer[:, rows + 2, where, :] = value
+            buffer[:, rows + 3, where, :] = value
+
+    sides = ((0, PAD, PAD + cells, wedges - 1), (1, PAD + cells - 2, PAD - 2, 1))
+
+    def phi_copies(source, target, slot):
         return [
             remote(
-                edge.at[slot + side, :, pl.ds(0, count)],
-                halo.at[slot + side, :, pl.ds(0, count)],
-                phi_send.at[section], phi_recv.at[section], phi_peer(jump),
+                source.at[side], target.at[side], phi_send.at[slot], phi_recv.at[slot],
+                phi_peer(jump),
             )
-            for side, jump in ((0, wedges - 1), (1, 1))
+            for side, _, _, jump in sides
         ]
 
-    def phi_both(section, count):
-        where = (pl.ds(2 * section, 2), slice(None), pl.ds(0, count))
-        return remote(
-            edge.at[where], halo.at[where], phi_send.at[section], phi_recv.at[section],
-            phi_peer(1),
-        )
-
-    def phi_pack(buffer, section, pieces):
-        for side, start in ((0, PAD), (1, PAD + cells - 2)):
-            at = 0
-            for begin, count in pieces:
-                edge[section * 2 + side, :, pl.ds(at, count)] = buffer[
-                    :, pl.ds(2 + begin, count), pl.ds(start, 2), :
-                ]
-                at += count
-
-    def phi_unpack(buffer, section, pieces):
-        for side, start in ((0, PAD + cells), (1, PAD - 2)):
-            at = 0
-            for begin, count in pieces:
-                buffer[:, pl.ds(2 + begin, count), pl.ds(start, 2), :] = halo[
-                    section * 2 + side, :, pl.ds(at, count)
-                ]
-                at += count
+    def phi_both(source, target, slot):
+        return remote(source, target, phi_send.at[slot], phi_recv.at[slot], phi_peer(1))
+
+    def phi_pack(buffer, full, piece, begin, count):
+        for side, start, _, _ in sides:
+            for i in range(count):
+                value = buffer[:, 2 + begin + i, pl.ds(start, 2), :]
+                piece[side, :, :, i, :] = value
+                if full is not None:
+                    full[side, :, :, begin + i, :] = value
+
+    def phi_unpack(buffer, full, piece, begin, count):
+        for side, _, start, _ in sides:
+            for i in range(count):
+                value = piece[side, :, :, i, :]
+                buffer[:, 2 + begin + i, pl.ds(start, 2), :] = value
+                if full is not None:
+                    full[side, :, :, begin + i, :] = value
 
     lane = lax.broadcasted_iota(jnp.int32, (rows, lanes), 1)
     line = lax.broadcasted_iota(jnp.int32, (rows, lanes), 0)
@@ -415,7 +413,7 @@
     ) * radial_step
     column = column * centres * centres * (radial_step * theta_step * phi_step)
     part[...] = jnp.sum(jnp.where(lane == line, column, 0.0), axis=0, keepdims=True)
-    phi_pack(first, 0, whole)
+    phi_pack(first, None, edge_one, 0, rows)
 
     on = stencils(sizes, input_ref.shape, slab, table, ends, radial)
 
@@ -458,8 +456,8 @@
         got_part.at[others], got_part.at[others], part_send.at[0], part_recv.at[0], phi_peer(1)
     )
     first_radial, second_radial = radial_copies(first, 0), radial_copies(second, 1)
-    first_phi = phi_copies(0, rows)
-    inside_phi, edge_phi = phi_copies(1, rows - 4), phi_copies(2, 4)
+    first_phi = phi_copies(edge_one, halo_one, 0)
+    inside_phi = phi_copies(edge_inside, halo_inside, 1)
     for copy in part_copies:
         copy.start()
     radial_start(first_radial)
@@ -521,39 +519,61 @@
                 pl.semaphore_wait(far.at[at], heard[at])
                 each_slab(low, high, slab_start)
 
-    phi_both(0, rows).wait_recv()
-    phi_unpack(first, 0, whole)
-    on.phi_ends(first)
+    def edge_rows(number, high):
+        up, down = first_radial
+        second_up, second_down = second_radial
+        begin = jnp.where(high, rows - 2, 0)
+        low = jnp.logical_not(high)
+        pl.when(jnp.logical_and(high, has_up))(down.wait_recv)
+        pl.when(jnp.logical_and(low, has_down))(up.wait_recv)
+        pl.when(jnp.logical_and(high, jnp.logical_not(has_up)))(lambda: top_end(first))
+        pl.when(jnp.logical_and(low, jnp.logical_not(has_down)))(lambda: bottom_end(first))
+        on.radial_store(first, jnp.where(high, rows - 1, 0), 2)
+        each(begin, begin + 2, late_one)
+
+        @pl.when(jnp.logical_and(high, has_up))
+        def _():
+            up.wait_send()
+            second_up.start()
+
+        @pl.when(jnp.logical_and(low, has_down))
+        def _():
+            down.wait_send()
+            second_down.start()
+
+        phi_pack(second, edge_two, edge_end.at[number], begin, 2)
+        for copy in phi_copies(edge_end.at[number], halo_end.at[number], 2 + number):
+            copy.start()
+
+    phi_both(edge_one, halo_one, 0).wait_recv()
+    phi_unpack(first, None, halo_one, 0, rows)
+    on.phi_ends(edge_one, halo_one, lambda k, side, cell, other, value: value)
     each(2, rows - 2, late_one)
-    phi_pack(second, 1, inside_rows)
+    phi_pack(second, edge_two, edge_inside, 2, rows - 4)
     for copy in inside_phi:
         copy.start()
+    edge_rows(0, c == 0)
     pl.when(turns)(send_out)
-    radial_land(first_radial)
-    radial_ends(first)
-    each(0, 2, lambda i: on.radial_store(first, 7 * i, 2))
-    each(0, 4, lambda i: late_one(i + (i // 2) * (rows - 4)))
-    radial_sent(first_radial)
-    radial_start(second_radial)
-    phi_pack(second, 2, edge_rows)
-    for copy in edge_phi:
-        copy.start()
+    edge_rows(1, c == 1)
     pl.when(jnp.logical_not(turns))(send_out)
 
     after = jnp.where(lane < line, 1.0, jnp.where(lane == line, 0.5, 0.0))
     within = jnp.sum(after * slab_part[...], axis=1, keepdims=True)
     whole = jnp.sum(jnp.where(line >= 0, slab_part[...], 0.0), axis=1, keepdims=True)
 
-    phi_both(1, rows - 4).wait_recv()
-    phi_unpack(second, 1, inside_rows)
-    phi_both(2, 4).wait_recv()
-    phi_unpack(second, 2, edge_rows)
+    phi_both(edge_inside, halo_inside, 1).wait_recv()
+    phi_unpack(second, halo_two, halo_inside, 2, rows - 4)
+    for number in range(2):
+        begin = jnp.where(c == number, rows - 2, 0)
+        phi_both(edge_end.at[number], halo_end.at[number], 2 + number).wait_recv()
+        phi_unpack(second, halo_two, halo_end.at[number], begin, 2)
     radial_land(second_radial)
 
     part_all.wait_send()
-    phi_both(0, rows).wait_send()
-    phi_both(1, rows - 4).wait_send()
-    phi_both(2, 4).wait_send()
+    phi_both(edge_one, halo_one, 0).wait_send()
+    phi_both(edge_inside, halo_inside, 1).wait_send()
+    for number in range(2):
+        phi_both(edge_end.at[number], halo_end.at[number], 2 + number).wait_send()
     radial_sent(second_radial)
     by_slab(0, slabs, lambda s: slab_all(slabs - max(s, 1)).wait_send())
     pl.when(has_up)(above_copy.wait_recv)
@@ -585,7 +605,20 @@
             pulled(row, PAD + TILE * t)
 
     each_pair(0, rows + 4, pulled_row)
-    radial_ends(second)
+    pl.when(jnp.logical_not(has_down))(lambda: bottom_end(second))
+    pl.when(jnp.logical_not(has_up))(lambda: top_end(second))
+
+    tug = timestep * pull[pl.ds(TILE, rows), :]
+
+    def pulled_end(k, side, cell, other, value):
+        begin = halo_one if other else edge_one
+        if k == 1:
+            value = value - jnp.maximum(begin[side, 0, cell], MINIMUM_DENSITY) * tug
+        if k == 4:
+            value = value - begin[side, 1, cell] * tug
+        return value
+
+    on.phi_ends(edge_two, halo_two, pulled_end)
 
 
 def finish(
@@ -595,10 +628,10 @@
     pull,
     table,
     mass,
+    ends,
     out_ref,
     mass_ref,
     out,
-    ends,
     radial,
     sem,
 ):
@@ -645,7 +678,6 @@
         section_two(2 * i + 1)
         save(i).start()
 
-    on.phi_ends(second)
     each(0, (rows + 1) // 3, lambda i: on.radial_store(second, 3 * i, 3))
     each(0, rows // 2, two)
     pltpu.make_async_copy(out, out_ref, sem.at[0]).wait()
@@ -660,7 +692,7 @@
     padded = (variables, rows + 4, cells + 2 * PAD, lanes)
     vmem = pl.BlockSpec(memory_space=pltpu.VMEM)
     dma = pltpu.SemaphoreType.DMA
-    first, second, pull, table, mass = pl.pallas_call(
+    first, second, pull, table, mass, ends = pl.pallas_call(
         functools.partial(kernel, sizes, (slabs, wedges)),
         out_shape=(
             pltpu.VMEM(padded, jnp.float32),
@@ -668,14 +700,15 @@
             pltpu.VMEM((3 * TILE, lanes), jnp.float32),
             pltpu.VMEM((TILE, lanes), jnp.float32),
             pltpu.VMEM((1, rows), jnp.float32),
+            pltpu.VMEM((2, variables, rows, lanes), jnp.float32),
         ),
         in_specs=[pl.BlockSpec(memory_space=pl.ANY)] * 3,
-        out_specs=(vmem,) * 5,
+        out_specs=(vmem,) * 6,
         scratch_shapes=[
-            pltpu.VMEM((6, variables, rows, 2, lanes), jnp.float32),
-            pltpu.VMEM((6, variables, rows, 2, lanes), jnp.float32),
+            *[pltpu.VMEM((2, variables, 2, rows, lanes), jnp.float32)] * 4,
+            *[pltpu.VMEM((2, variables, 2, rows - 4, lanes), jnp.float32)] * 2,
+            *[pltpu.VMEM((2, 2, variables, 2, 2, lanes), jnp.float32)] * 2,
             pltpu.VMEM((variables, rows + 1, cells, lanes), jnp.float32),
-            pltpu.VMEM((2, variables, rows, lanes), jnp.float32),
             pltpu.VMEM((1, lanes), jnp.float32),
             pltpu.VMEM((1, lanes), jnp.float32),
             pltpu.VMEM((wedges, 1, lanes), jnp.float32),
@@ -687,8 +720,8 @@
             dma((3,)),
             dma((2,)),
             dma((4,)),
-            dma((3,)),
-            dma((3,)),
+            dma((4,)),
+            dma((4,)),
             dma((1,)),
             dma((1,)),
             dma((1,)),
@@ -703,16 +736,15 @@
             jax.ShapeDtypeStruct(conserved.shape, jnp.float32),
             jax.ShapeDtypeStruct((1, rows), jnp.float32),
         ),
-        in_specs=[vmem] * 5,
+        in_specs=[vmem] * 6,
         out_specs=(pl.BlockSpec(memory_space=pltpu.HBM),) * 2,
         scratch_shapes=[
             pltpu.VMEM(conserved.shape, jnp.float32),
-            pltpu.VMEM((2, variables, rows, lanes), jnp.float32),
             pltpu.VMEM((variables, rows + 1, cells, lanes), jnp.float32),
             dma((2,)),
         ],
         compiler_params=pltpu.CompilerParams(vmem_limit_bytes=16 * 1024 * 1024),
-    )(first, second, pull, table, mass)
+    )(first, second, pull, table, mass, ends)
     return advanced, mass.reshape(rows)
 
 

time: 22.8 us -> 22.1 us (0.969)
  Pallas kernels: 21.4 us -> 20.7 us
    pallas_call x1, Pallas kernels: 18.2 us -> 17.8 us  [body(): pl.pallas_call(functools.partial(kernel, sizes, (slabs, wedges)), out_sha...]
    pallas_call x1, Pallas kernels: 3.21 us -> 2.91 us  [body(): pl.pallas_call(functools.partial(finish, sizes), out_shape=(jax.ShapeDtyp...]
where the time goes in v5:
time: 22.1 us; the launch traced here: 22 us
  Pallas kernels  20.7 us (94%)
  between operations  1.28 us (6%)
    pallas_call x1, Pallas kernels, body(): pl.pallas_call(functools.partial(kernel, sizes, (slabs, wedges)), out_sha...  17.8 us
    pallas_call x1, Pallas kernels, body(): pl.pallas_call(functools.partial(finish, sizes), out_shape=(jax.ShapeDtyp...  2.91 us

profile of v5, /device:TPU:2, one launch (start us, length us, event | category | flops | bytes accessed | tf_op | source)
XLA Modules:
  0.0 22.0 jit_solution(10075063700395965737)
XLA Ops:
  1.3 17.8 %shard_map.50 = (f32[8,12,32,128]{3,2,1,0:T(8,128)S(1)}, f32[8,12,32,128]{3,2,1,0:T(8,128)S(1)}, f32[24,128]{1,0:T(8,128)S(1)}, f32[8,128]{1,0:T(8,128)S(1)}, f3...) custom-call(f32[1]{0:T(128)S(6)} %copy.5.core_ref, f32[8,128]{1,0:T(8,128)} %constant.2.clone.table_ref, ...), custom_call_target="tpu_custom_call" | custom-call | tf_op jit(solution)/shard_map/pallas_call | solution.py:695
  19.1 2.9 %shard_map.51 = (f32[8,8,16,128]{3,2,1,0:T(8,128)}, f32[1,8]{1,0:T(1,128)}) custom-call(f32[8,12,32,128]{3,2,1,0:T(8,128)S(1)} %get-tuple-element.10.first, f32[8,12,32,128]{3,2,1,0:T(8,128)S(1)} %get-tuple-element.11.second, f32[24,128]{1,0:T(8,128)S(1)} %get-tuple-element.12.pull, f32[8,128]{1,0:T(8,128)S(1)} %get-tuple-element.13.table, ...), custom_call_target="tpu_custom_call" | custom-call | tf_op jit(solution)/shard_map/pallas_call | solution.py:733

commit v6 on v5

--- a/solution.py
+++ b/solution.py
@@ -22,6 +22,7 @@
 PAD = 8
 DEPTH = 8
 LINE = 2 * DEPTH
+STEP = 4
 TOP = 4
 
 
@@ -291,22 +292,34 @@
         pl.semaphore_signal(semaphore, inc=1, device_id=peer, device_id_type=MESH)
 
     def each_slab(low, high, step):
-        def one_level(at):
+        def spread_out(at):
             for i in range(span):
-                spread_out = LINE * (i // 2) + 2 * at + i % 2
-                step(jnp.where(at < TOP, spread_out, LINE * (at - TOP) + LINE // 2 + i))
-
-        each(low, high, one_level)
+                step(2 * at + LINE * (i // 2) + i % 2, False)
+
+        def block(at):
+            for i in range(span):
+                last = i // 2 == DEPTH - TOP - 1
+                step(LINE * at + (LINE // 2 - LINE * TOP + i), i % 2 == (1 if last else 0))
+
+        each(low, jnp.minimum(high, TOP), spread_out)
+        each(jnp.maximum(low, TOP), high, block)
 
     def greet(v):
         signal(barrier, (v, wedge))
 
-    def greet_level(v):
-        pl.when(jnp.logical_or(v < slab, v == slab + 1))(lambda: greet(v))
-
-    def greet_outer(v):
-        known = jnp.logical_or(v % LINE != LINE - 1, v == slab - 1)
+    def near(v):
+        return jnp.logical_or(v == slab + 1, v == slab - 1)
+
+    def greet_level(v, later):
+        known = jnp.logical_or(v < slab, v == slab + 1)
+        known = jnp.logical_and(known, near(v)) if later else known
         pl.when(known)(lambda: greet(v))
+
+    def greet_outer(v, later):
+        if later:
+            pl.when(near(v))(lambda: greet(v))
+        else:
+            greet(v)
 
     for j in range(1, wedges):
         signal(barrier, phi_peer(j))
@@ -315,7 +328,8 @@
     each_slab(level, level + 1, greet_level)
     each_slab(level + 1, levels, greet_outer)
     inside = jnp.where(z < TOP, 2 * c, jnp.where(rank > 0, 1, 0))
-    inside = jnp.where(turned_last, jnp.where(has_up, 2, 1), span * level + span - 1 - rank + inside)
+    late = jnp.logical_and(z >= TOP, c == jnp.where(z == DEPTH - 1, 1, 0))
+    inside = jnp.where(late, jnp.where(has_up, 2, 1), span * level + span - 1 - rank + inside)
     greeted = (wedges - 1) + inside + jnp.where(turns, 1, 0)
     further = slabs // LINE - 1 - x
     heard = (
@@ -323,9 +337,6 @@
         jnp.where(z < TOP, (DEPTH - TOP) * 2 * (further + 1), span * further),
     )
 
-    load.wait()
-    load_table.wait()
-    load_core.wait()
 
     def remote(src, dst, send, recv, peer):
         return pltpu.make_async_remote_copy(
@@ -345,11 +356,6 @@
         )
         return up, down
 
-    def radial_start(copies):
-        up, down = copies
-        pl.when(has_up)(up.start)
-        pl.when(has_down)(down.start)
-
     def radial_sent(copies):
         up, down = copies
         pl.when(has_up)(up.wait_send)
@@ -404,6 +410,16 @@
                 if full is not None:
                     full[side, :, :, begin + i, :] = value
 
+    first_radial, second_radial = radial_copies(first, 0), radial_copies(second, 1)
+    load.wait()
+
+    @pl.when(turned_last)
+    def _():
+        pl.semaphore_wait(barrier, greeted)
+        pl.when(has_up)(first_radial[0].start)
+
+    load_table.wait()
+    load_core.wait()
     lane = lax.broadcasted_iota(jnp.int32, (rows, lanes), 1)
     line = lax.broadcasted_iota(jnp.int32, (rows, lanes), 0)
     column = jnp.sum(first[0, pl.ds(2, rows), pl.ds(PAD, cells), :], axis=1)
@@ -442,9 +458,9 @@
                     second[k, r + 2, where, :] + part_of[k] * around + across * along
                 )
 
-    pl.semaphore_wait(barrier, greeted)
-
-    def reply(v):
+    pl.when(jnp.logical_not(turned_last))(lambda: pl.semaphore_wait(barrier, greeted))
+
+    def reply(v, _):
         pl.when(v < slab)(lambda: signal(far.at[jnp.where(z < TOP, 0, 1)], (v, wedge)))
 
     part_copies = [
@@ -455,31 +471,32 @@
     part_all = remote(
         got_part.at[others], got_part.at[others], part_send.at[0], part_recv.at[0], phi_peer(1)
     )
-    first_radial, second_radial = radial_copies(first, 0), radial_copies(second, 1)
     first_phi = phi_copies(edge_one, halo_one, 0)
     inside_phi = phi_copies(edge_inside, halo_inside, 1)
     for copy in part_copies:
         copy.start()
-    radial_start(first_radial)
+    pl.when(jnp.logical_and(has_up, jnp.logical_not(turned_last)))(first_radial[0].start)
+    pl.when(has_down)(first_radial[1].start)
     for copy in first_phi:
         copy.start()
 
-    pl.when(slab % LINE == LINE - 2)(lambda: signal(told, (slab + 1, wedge)))
-
-    @pl.when(jnp.logical_not(turned_last))
+    teller = jnp.logical_and(z >= TOP, jnp.logical_not(late))
+    pl.when(teller)(lambda: signal(told, (slab + 1 - 2 * c, wedge)))
+
+    @pl.when(jnp.logical_not(late))
     def _():
         each_slab(0, level, reply)
 
     got_part[0] = part[...]
     each_pair(0, rows, early_one)
-    each(0, 2, lambda i: on.radial_store(first, 2 + 2 * i, 2))
-    on.radial_store(first, 6, 1)
-
-    @pl.when(turned_last)
+
+    @pl.when(late)
     def _():
         pl.semaphore_wait(told, 1)
         each_slab(0, level, reply)
 
+    each(0, 2, lambda i: on.radial_store(first, 2 + 2 * i, 2))
+    on.radial_store(first, 6, 1)
     part_all.wait_recv()
     shells = jnp.zeros((1, lanes), jnp.float32)
     for w in range(wedges):
@@ -503,7 +520,7 @@
         pl.when(slab < middle)(lambda: by_slab(low, middle, step))
         pl.when(slab >= middle)(lambda: by_slab(middle, high, step))
 
-    def slab_start(v):
+    def slab_start(v, _):
         pl.when(v > slab)(lambda: slab_copy(slab, v).start())
 
     above_copy = remote(
@@ -553,9 +570,8 @@
     for copy in inside_phi:
         copy.start()
     edge_rows(0, c == 0)
-    pl.when(turns)(send_out)
     edge_rows(1, c == 1)
-    pl.when(jnp.logical_not(turns))(send_out)
+    send_out()
 
     after = jnp.where(lane < line, 1.0, jnp.where(lane == line, 0.5, 0.0))
     within = jnp.sum(after * slab_part[...], axis=1, keepdims=True)
@@ -670,16 +686,16 @@
                 out[k, r, into, :] = total[k]
 
     def save(i):
-        where = (slice(None), pl.ds(2 * i, 2))
+        where = (slice(None), pl.ds(STEP * i, STEP))
         return pltpu.make_async_copy(out.at[where], out_ref.at[where], sem.at[0])
 
-    def two(i):
-        section_two(2 * i)
-        section_two(2 * i + 1)
+    def several(i):
+        for j in range(STEP):
+            section_two(STEP * i + j)
         save(i).start()
 
     each(0, (rows + 1) // 3, lambda i: on.radial_store(second, 3 * i, 3))
-    each(0, rows // 2, two)
+    each(0, rows // STEP, several)
     pltpu.make_async_copy(out, out_ref, sem.at[0]).wait()
     save_mass.wait()
 

time: 22.1 us -> 21 us (0.950)
  Pallas kernels: 20.7 us -> 19.5 us
    pallas_call x1, Pallas kernels: 17.8 us -> 16.9 us  [body(): pl.pallas_call(functools.partial(kernel, sizes, (slabs, wedges)), out_sha...]
    pallas_call x1, Pallas kernels: 2.91 us -> 2.61 us  [body(): pl.pallas_call(functools.partial(finish, sizes), out_shape=(jax.ShapeDtyp...]
where the time goes in v6:
time: 21 us; the launch traced here: 20.8 us
  Pallas kernels  19.5 us (93%)
  between operations  1.28 us (6%)
    pallas_call x1, Pallas kernels, body(): pl.pallas_call(functools.partial(kernel, sizes, (slabs, wedges)), out_sha...  16.9 us
    pallas_call x1, Pallas kernels, body(): pl.pallas_call(functools.partial(finish, sizes), out_shape=(jax.ShapeDtyp...  2.61 us

profile of v6, /device:TPU:2, one launch (start us, length us, event | category | flops | bytes accessed | tf_op | source)
XLA Modules:
  0.0 20.8 jit_solution(3679842161191508927)
XLA Ops:
  1.3 16.9 %shard_map.50 = (f32[8,12,32,128]{3,2,1,0:T(8,128)S(1)}, f32[8,12,32,128]{3,2,1,0:T(8,128)S(1)}, f32[24,128]{1,0:T(8,128)S(1)}, f32[8,128]{1,0:T(8,128)S(1)}, f3...) custom-call(f32[1]{0:T(128)S(6)} %copy.5.core_ref, f32[8,128]{1,0:T(8,128)} %constant.2.clone.table_ref, ...), custom_call_target="tpu_custom_call" | custom-call | tf_op jit(solution)/shard_map/pallas_call | solution.py:711
  18.2 2.6 %shard_map.51 = (f32[8,8,16,128]{3,2,1,0:T(8,128)}, f32[1,8]{1,0:T(1,128)}) custom-call(f32[8,12,32,128]{3,2,1,0:T(8,128)S(1)} %get-tuple-element.10.first, f32[8,12,32,128]{3,2,1,0:T(8,128)S(1)} %get-tuple-element.11.second, f32[24,128]{1,0:T(8,128)S(1)} %get-tuple-element.12.pull, f32[8,128]{1,0:T(8,128)S(1)} %get-tuple-element.13.table, ...), custom_call_target="tpu_custom_call" | custom-call | tf_op jit(solution)/shard_map/pallas_call | solution.py:749

commit v7 on v6

--- a/solution.py
+++ b/solution.py
@@ -429,7 +429,6 @@
     ) * radial_step
     column = column * centres * centres * (radial_step * theta_step * phi_step)
     part[...] = jnp.sum(jnp.where(lane == line, column, 0.0), axis=0, keepdims=True)
-    phi_pack(first, None, edge_one, 0, rows)
 
     on = stencils(sizes, input_ref.shape, slab, table, ends, radial)
 
@@ -475,6 +474,7 @@
     inside_phi = phi_copies(edge_inside, halo_inside, 1)
     for copy in part_copies:
         copy.start()
+    phi_pack(first, None, edge_one, 0, rows)
     pl.when(jnp.logical_and(has_up, jnp.logical_not(turned_last)))(first_radial[0].start)
     pl.when(has_down)(first_radial[1].start)
     for copy in first_phi:
@@ -694,7 +694,8 @@
             section_two(STEP * i + j)
         save(i).start()
 
-    each(0, (rows + 1) // 3, lambda i: on.radial_store(second, 3 * i, 3))
+    for i in range((rows + 1) // 3):
+        on.radial_store(second, 3 * i, 3)
     each(0, rows // STEP, several)
     pltpu.make_async_copy(out, out_ref, sem.at[0]).wait()
     save_mass.wait()

time: 21 us -> 21.2 us (level)
  the two profiles are of different devices: /device:TPU:2 before, /device:TPU:1 now
where the time goes in v7:
time: 21.2 us; the launch traced here: 21.1 us
  Pallas kernels  19.8 us (93%)
  between operations  1.28 us (6%)
    pallas_call x1, Pallas kernels, body(): pl.pallas_call(functools.partial(kernel, sizes, (slabs, wedges)), out_sha...  17.2 us
    pallas_call x1, Pallas kernels, body(): pl.pallas_call(functools.partial(finish, sizes), out_shape=(jax.ShapeDtyp...  2.57 us

profile of v7, /device:TPU:1, one launch (start us, length us, event | category | flops | bytes accessed | tf_op | source)
XLA Modules:
  0.0 21.1 jit_solution(7582478467863806889)
XLA Ops:
  1.3 17.2 %shard_map.50 = (f32[8,12,32,128]{3,2,1,0:T(8,128)S(1)}, f32[8,12,32,128]{3,2,1,0:T(8,128)S(1)}, f32[24,128]{1,0:T(8,128)S(1)}, f32[8,128]{1,0:T(8,128)S(1)}, f3...) custom-call(f32[1]{0:T(128)S(6)} %copy.5.core_ref, f32[8,128]{1,0:T(8,128)} %constant.2.clone.table_ref, ...), custom_call_target="tpu_custom_call" | custom-call | tf_op jit(solution)/shard_map/pallas_call | solution.py:712
  18.5 2.6 %shard_map.51 = (f32[8,8,16,128]{3,2,1,0:T(8,128)}, f32[1,8]{1,0:T(1,128)}) custom-call(f32[8,12,32,128]{3,2,1,0:T(8,128)S(1)} %get-tuple-element.10.first, f32[8,12,32,128]{3,2,1,0:T(8,128)S(1)} %get-tuple-element.11.second, f32[24,128]{1,0:T(8,128)S(1)} %get-tuple-element.12.pull, f32[8,128]{1,0:T(8,128)S(1)} %get-tuple-element.13.table, ...), custom_call_target="tpu_custom_call" | custom-call | tf_op jit(solution)/shard_map/pallas_call | solution.py:750
